TPU v7x, 128 devices: a whole 4x4x4 slice. The times are simulated.
128 devices in a mesh: dp: 1, ep: 128 (over z, y, x, core).
Axes of the slice: x: 4, y: 4, z: 4, core: 2. Of those that a mesh axis runs over, the one named last changes fastest.
Arguments:
- x_rows: bfloat16 [65536, 2048], P(('dp', 'ep'))
- logits: float32 [65536, 128], P(('dp', 'ep'))
- w_in: bfloat16 [128, 2048, 768], P('ep')
- w_out: bfloat16 [128, 768, 2048], P('ep')
Outputs:
- output: bfloat16 [65536, 2048], P(('dp', 'ep'))
All inputs are finite; a program needn't handle non-finite values.
Results may differ from a plain program's by a relative error of at most 0.001.
Values are sent between devices in bfloat16 or wider.
A program may use at most 1 GiB of HBM per device.

v0:
```python
import jax
import jax.numpy as jnp
from jax import lax
from jax.sharding import PartitionSpec as P

CAP_FACTOR = 2


def solution(mesh):
    group_size = mesh.shape['ep']
    row_spec = P(('dp', 'ep'), None)
    expert_spec = P('ep', None, None)

    def local_step(x_rows, logits, w_in, w_out):
        tok_dev, d_model = x_rows.shape
        experts = logits.shape[1]
        exp_dev = w_in.shape[0]
        capacity = CAP_FACTOR * tok_dev * group_size // experts
        src_cap = 4 * tok_dev // experts
        my_index = lax.axis_index('ep')
        gate_probs = jax.nn.softmax(logits, axis=-1)
        top_vals, top_ids = lax.top_k(logits, 2)
        chosen = (logits >= top_vals[:, 1:2]).astype(jnp.int32)
        local_before = jnp.cumsum(chosen, axis=0) - chosen
        local_counts = jnp.sum(chosen, axis=0).astype(jnp.float32)
        all_counts = lax.all_gather(local_counts, 'ep').astype(jnp.int32)
        dev_offsets = jnp.cumsum(all_counts, axis=0) - all_counts
        local_pos = jnp.take_along_axis(local_before, top_ids, axis=1)
        kept_mask = local_pos + jnp.take(dev_offsets[my_index], top_ids) < capacity
        send_row = jnp.where(kept_mask, top_ids * src_cap + local_pos, experts * src_cap)
        tok_ids = jnp.broadcast_to(jnp.arange(tok_dev, dtype=jnp.int32)[:, None], (tok_dev, 2))
        slot_tok = jnp.full((experts * src_cap,), tok_dev, jnp.int32).at[send_row.reshape(-1)].set(tok_ids.reshape(-1), mode='drop')
        send_buf = jnp.take(x_rows, slot_tok, axis=0, mode='fill', fill_value=0)
        recv_buf = lax.all_to_all(send_buf, 'ep', 0, 0, tiled=True)

        own_counts = lax.dynamic_slice_in_dim(all_counts, my_index * exp_dev, exp_dev, axis=1)
        own_offsets = lax.dynamic_slice_in_dim(dev_offsets, my_index * exp_dev, exp_dev, axis=1)
        kept_counts = jnp.minimum(jnp.maximum(capacity - own_offsets, 0), own_counts)
        slot_ends = (own_offsets + kept_counts).T
        cap_ids = jnp.arange(capacity, dtype=jnp.int32)
        below_mask = slot_ends[:, None, :] <= cap_ids[None, :, None]
        src_dev = jnp.sum(below_mask.astype(jnp.int32), axis=2)
        slot_start = jnp.sum(jnp.where(below_mask, kept_counts.T[:, None, :], 0), axis=2)
        exp_local = jnp.arange(exp_dev, dtype=jnp.int32)
        recv_row = (src_dev * exp_dev + exp_local[:, None]) * src_cap + cap_ids[None, :] - slot_start
        recv_row = jnp.where(src_dev < group_size, recv_row, group_size * exp_dev * src_cap)
        expert_rows = jnp.take(recv_buf, recv_row.reshape(-1), axis=0, mode='fill', fill_value=0).reshape(exp_dev, capacity, d_model)
        hidden = jax.nn.gelu(jnp.einsum('ecd,edf->ecf', expert_rows, w_in, preferred_element_type=jnp.float32), approximate=True).astype(jnp.bfloat16)
        expert_out = jnp.einsum('ecf,efd->ecd', hidden, w_out, preferred_element_type=jnp.float32).astype(jnp.bfloat16).reshape(exp_dev * capacity, d_model)

        src_slots = jnp.arange(src_cap, dtype=jnp.int32)
        back_row = exp_local[None, :, None] * capacity + own_offsets[:, :, None] + src_slots[None, None, :]
        back_row = jnp.where(src_slots[None, None, :] < kept_counts[:, :, None], back_row, exp_dev * capacity)
        back_buf = jnp.take(expert_out, back_row.reshape(-1), axis=0, mode='fill', fill_value=0)
        ret_buf = lax.all_to_all(back_buf, 'ep', 0, 0, tiled=True)

        rows_back = jnp.take(ret_buf, send_row, axis=0, mode='fill', fill_value=0)
        pick_gate = jnp.take_along_axis(gate_probs, top_ids, axis=1)
        mix_sum = jnp.sum(pick_gate[:, :, None] * rows_back.astype(jnp.float32), axis=1)
        return (x_rows.astype(jnp.float32) + mix_sum).astype(jnp.bfloat16)

    return jax.shard_map(local_step, mesh=mesh, in_specs=(row_spec, row_spec, expert_spec, expert_spec), out_specs=row_spec, check_vma=False)
```

profile of v0, /device:TPU:12, one launch (start us, length us, event | category | flops | bytes accessed | tf_op | source)
XLA Modules:
  0.0 523.0 jit_solution(10776706517239773722)
XLA Ops:
  0.0 82.7 %top_k.7 = (f32[512,2]{1,0:T(8,128)}, s32[512,2]{1,0:T(8,128)S(1)}) custom-call(f32[512,128]{1,0:T(8,128)} %param.5), custom_call_target="TopK", called_computations={%compare_greater_than.1.1.clone.clone} | custom-call | tf_op jit(solution)/shard_map/top_k | solution.py:22
  84.9 1.7 reshape.474
  86.6 1.2 slice_reduce_fusion
  87.8 1.8 fusion.45
  89.6 35.5 %all-gather.1 = f32[128,1,128]{2,1,0:T(1,128)S(1)} all-gather(f32[1,1,128]{2,1,0:T(1,128)S(1)} %convert_bitcast_fusion), channel_id=2, replica_groups=mesh['dp'=1,'ep'=128] {'ep'}, dimensions={0}, use_global_device_ids=true | all-gather | bytes 66048 | tf_op jit(solution)/shard_map/all_gather | solution.py:26
  126.7 1.1 fusion.27
  128.6 1.0 broadcast_add_fusion
  129.6 1.0 bitcast_subtract_fusion
  130.6 1.1 reshape.458
  131.7 6.8 %gather_fusion.6 = s32[1024]{0:T(1024)S(1)} fusion(s32[512,128]{1,0:T(8,128)S(1)} %bitcast_subtract_fusion, s32[1024]{0:T(1024)S(1)} %reshape.458), kind=kCustom, calls=%fused_computation.6 | custom fusion | bytes 16384 | tf_op jit(solution)/shard_map/jit(take_along_axis)/gather | solution.py:28
  138.6 0.9 reshape.467
  139.5 1.1 reshape.420
  140.6 6.6 %gather_fusion = s32[1024]{0:T(1024)S(1)} fusion(s32[128]{0:T(128)S(1)} %fusion.38, s32[1024]{0:T(1024)S(1)} %broadcast_clamp_fusion.3), kind=kCustom, calls=%fused_computation | custom fusion | bytes 12288 | tf_op jit(solution)/shard_map/jit(_take)/gather | solution.py:29
  147.2 0.9 reshape.419
  148.1 1.9 compare_and_fusion
  150.0 1.1 reshape.414
  151.2 4.5 scatter_custom_fusion
  155.8 18.2 %gather_fusion.1 = bf16[2048,2048]{1,0:T(8,128)(2,1)} fusion(bf16[512,2048]{1,0:T(8,128)(2,1)} %param.4, s32[2048]{0:T(1024)S(1)} %fusion.35), kind=kCustom, calls=%fused_computation.1 | custom fusion | bytes 16785408 | tf_op jit(solution)/shard_map/jit(_take)/gather | solution.py:33
  174.0 7.3 %broadcast_select_fusion = bf16[128,16,2048]{2,1,0:T(8,128)(2,1)} fusion(bf16[128,16,2048]{2,1,0:T(8,128)(2,1)} %bitcast.71, pred[128,16]{1,0:T(8,128)(4,1)S(1)} %broadcast_in_dim.115), kind=kLoop, calls=%fused_computation.9 | loop fusion | flops 4194304 | bytes 16779264 | tf_op jit(solution)/shard_map/jit(_take)/select_n | solution.py:33
  181.2 8.4 %all-to-all-start = ((bf16[128,16,2048]{2,1,0:T(8,128)(2,1)}), bf16[128,16,2048]{2,1,0:T(8,128)(2,1)}, u32[]{:S(2)}, u32[]{:S(2)}) async-start(bf16[128,16,2048]{2,1,0:T(8,128)(2,1)} %broadcast_select_fusion), calls=%async_computation | async-start | bytes 16777216 | tf_op jit(solution)/shard_map/all_to_all | solution.py:34
  190.6 107.7 %all-to-all-done = bf16[128,16,2048]{2,1,0:T(8,128)(2,1)} async-done(((bf16[128,16,2048]{2,1,0:T(8,128)(2,1)}), bf16[128,16,2048]{2,1,0:T(8,128)(2,1)}, u32[]{:S(2)}, u32[]{:S(2)}) %all-to-all-start) | async-done | bytes 8388640 | tf_op jit(solution)/shard_map/all_to_all | solution.py:34
  298.3 13.3 %gather_fusion.2 = bf16[1024,2048]{1,0:T(8,128)(2,1)} fusion(bf16[2048,2048]{1,0:T(8,128)(2,1)} %bitcast.13, s32[1024]{0:T(1024)S(1)} %broadcast_clamp_fusion.2), kind=kCustom, calls=%fused_computation.2 | custom fusion | bytes 8392704 | tf_op jit(solution)/shard_map/jit(_take)/gather | solution.py:47
  311.6 12.2 %convolution_convert_fusion = bf16[1024,2048]{1,0:T(8,128)(2,1)} fusion(bf16[1,768,2048]{2,1,0:T(8,128)(2,1)S(1)} %copy-done, bf16[1024,2048]{1,0:T(8,128)(2,1)} %gather_fusion.2, pred[1024]{0:T(1024)(128)(4,1)S(1)} %get-tuple-element.20, bf16[1,2048,768]{2,1,0:T(8,128)(2,1)} %param.6), kind=kOutput, calls=%fused_computation.18 | convolution fusion | flops 6453723136 | bytes 14681088 | tf_op jit(solution)/shard_map/ecf,efd->ecd/dot_general | solution.py:49
  323.8 19.1 %gather_fusion.3 = bf16[2048,2048]{1,0:T(8,128)(2,1)} fusion(bf16[1024,2048]{1,0:T(8,128)(2,1)} %convolution_convert_fusion, s32[2048]{0:T(1024)S(1)} %broadcast_clamp_fusion), kind=kCustom, calls=%fused_computation.3 | custom fusion | bytes 16785408 | tf_op jit(solution)/shard_map/jit(_take)/gather | solution.py:54
  342.9 7.3 %broadcast_select_fusion.1 = bf16[128,16,2048]{2,1,0:T(8,128)(2,1)} fusion(bf16[128,16,2048]{2,1,0:T(8,128)(2,1)} %bitcast.70, pred[128,16]{1,0:T(8,128)(4,1)S(1)} %fusion.33), kind=kLoop, calls=%fused_computation.10 | loop fusion | flops 4194304 | bytes 16779264 | tf_op jit(solution)/shard_map/jit(_take)/select_n | solution.py:54
  350.1 14.5 %all-to-all-start.1 = ((bf16[128,16,2048]{2,1,0:T(8,128)(2,1)}), bf16[128,16,2048]{2,1,0:T(8,128)(2,1)}, u32[]{:S(2)}, u32[]{:S(2)}) async-start(bf16[128,16,2048]{2,1,0:T(8,128)(2,1)} %broadcast_select_fusion.1), calls=%async_computation.1 | async-start | bytes 16777216 | tf_op jit(solution)/shard_map/all_to_all | solution.py:55
  365.2 6.8 %gather_fusion.5 = f32[1024]{0:T(1024)S(1)} fusion(f32[512,128]{1,0:T(8,128)S(1)} %fusion.29, s32[1024]{0:T(1024)S(1)} %copy-done.4), kind=kCustom, calls=%fused_computation.5 | custom fusion | bytes 16384 | tf_op jit(solution)/shard_map/jit(take_along_axis)/gather | solution.py:58
  372.5 108.4 %all-to-all-done.1 = bf16[128,16,2048]{2,1,0:T(8,128)(2,1)} async-done(((bf16[128,16,2048]{2,1,0:T(8,128)(2,1)}), bf16[128,16,2048]{2,1,0:T(8,128)(2,1)}, u32[]{:S(2)}, u32[]{:S(2)}) %all-to-all-start.1) | async-done | bytes 8388640 | tf_op jit(solution)/shard_map/all_to_all | solution.py:55
  480.9 13.3 %gather_fusion.4 = bf16[1024,2048]{1,0:T(8,128)(2,1)} fusion(bf16[2048,2048]{1,0:T(8,128)(2,1)} %bitcast.23, s32[1024]{0:T(1024)S(1)} %broadcast_clamp_fusion.1), kind=kCustom, calls=%fused_computation.4 | custom fusion | bytes 8392704 | tf_op jit(solution)/shard_map/jit(_take)/gather | solution.py:57
  494.2 7.7 %reshape.451 = bf16[512,2,2048]{2,1,0:T(2,128)(2,1)} reshape(bf16[1024,2048]{1,0:T(8,128)(2,1)} %gather_fusion.4) | data formatting | bytes 8388608 | tf_op jit(solution)/shard_map/jit(_take)/gather | solution.py:57
  501.9 19.0 %multiply_reduce_fusion = f32[512,2048]{1,0:T(8,128)S(1)} fusion(bf16[512,2,2048]{2,1,0:T(2,128)(2,1)} %reshape.451, pred[512,2]{1,0:T(8,128)(4,1)S(1)} %copy-done.13, f32[512,2]{1,0:T(8,128)S(1)} %broadcast_select_fusion.3), kind=kLoop, calls=%fused_computation.8 | loop fusion | flops 7340032 | bytes 8393728 | tf_op jit(solution)/shard_map/reduce_sum | solution.py:59
  520.9 2.1 add_convert_fusion
  (66 shorter events, 6.8 us)
Async XLA Ops:
  0.0 311.6 %copy-start = (bf16[1,768,2048]{2,1,0:T(8,128)(2,1)S(1)}, bf16[1,768,2048]{2,1,0:T(8,128)(2,1)}, u32[]{:S(2)}) copy-start(bf16[1,768,2048]{2,1,0:T(8,128)(2,1)} %param.7) | copy-start | bytes 9437188
  82.7 46.9 %copy-start.6 = (s32[512,2]{1,0:T(8,128)}, s32[512,2]{1,0:T(8,128)S(1)}, u32[]{:S(2)}) copy-start(s32[512,2]{1,0:T(8,128)S(1)} %get-tuple-element.11) | copy-start | bytes 12292
  125.1 4.5 copy-start.11
  127.9 0.7 copy-start.10
  131.7 6.8 %copy-start.3 = (s32[1024]{0:T(1024)}, s32[1024]{0:T(1024)S(1)}, u32[]{:S(2)}) copy-start(s32[1024]{0:T(1024)S(1)} %reshape.458) | copy-start | bytes 12292
  140.6 7.5 %copy-start.7 = (s32[512,2]{1,0:T(8,128)S(1)}, s32[512,2]{1,0:T(8,128)}, u32[]{:S(2)}) copy-start(s32[512,2]{1,0:T(8,128)} %copy-done.6) | copy-start | bytes 12292
  181.2 8.4 %copy-start.12 = (f32[128,1,128]{2,1,0:T(1,128)S(1)}, f32[128,1,128]{2,1,0:T(1,128)}, u32[]{:S(2)}) copy-start(f32[128,1,128]{2,1,0:T(1,128)} %copy-done.11) | copy-start | bytes 196612
  181.2 117.1 %all-to-all-start = ((bf16[128,16,2048]{2,1,0:T(8,128)(2,1)}), bf16[128,16,2048]{2,1,0:T(8,128)(2,1)}, u32[]{:S(2)}, u32[]{:S(2)}) async-start(bf16[128,16,2048]{2,1,0:T(8,128)(2,1)} %broadcast_select_fusion), calls=%async_computation | async-start | bytes 16777216 | tf_op jit(solution)/shard_map/all_to_all | solution.py:34
  350.1 14.5 %copy-start.5 = (f32[512,128]{1,0:T(8,128)S(1)}, f32[512,128]{1,0:T(8,128)}, u32[]{:S(2)}) copy-start(f32[512,128]{1,0:T(8,128)} %param.5) | copy-start | bytes 786436
  350.1 15.1 %copy-start.4 = (s32[1024]{0:T(1024)S(1)}, s32[1024]{0:T(1024)}, u32[]{:S(2)}) copy-start(s32[1024]{0:T(1024)} %copy-done.3) | copy-start | bytes 12292
  350.1 130.8 %all-to-all-start.1 = ((bf16[128,16,2048]{2,1,0:T(8,128)(2,1)}), bf16[128,16,2048]{2,1,0:T(8,128)(2,1)}, u32[]{:S(2)}, u32[]{:S(2)}) async-start(bf16[128,16,2048]{2,1,0:T(8,128)(2,1)} %broadcast_select_fusion.1), calls=%async_computation.1 | async-start | bytes 16777216 | tf_op jit(solution)/shard_map/all_to_all | solution.py:55
  365.2 7.0 %copy-start.9 = (s32[512,2]{1,0:T(8,128)S(1)}, s32[512,2]{1,0:T(8,128)}, u32[]{:S(2)}) copy-start(s32[512,2]{1,0:T(8,128)} %get-tuple-element.19) | copy-start | bytes 12292
  365.2 7.2 %copy-start.8 = (s32[512,2]{1,0:T(8,128)S(1)}, s32[512,2]{1,0:T(8,128)}, u32[]{:S(2)}) copy-start(s32[512,2]{1,0:T(8,128)} %copy-done.6) | copy-start | bytes 12292
  494.2 7.7 %copy-start.13 = (pred[512,2]{1,0:T(8,128)(4,1)S(1)}, pred[512,2]{1,0:T(8,128)(4,1)}, u32[]{:S(2)}) copy-start(pred[512,2]{1,0:T(8,128)(4,1)} %get-tuple-element.18) | copy-start | bytes 3076
  501.9 19.0 %copy-start.2 = (bf16[512,2048]{1,0:T(8,128)(2,1)S(1)}, bf16[512,2048]{1,0:T(8,128)(2,1)}, u32[]{:S(2)}) copy-start(bf16[512,2048]{1,0:T(8,128)(2,1)} %param.4) | copy-start | bytes 6291460
  501.9 21.1 %copy-start.1 = (bf16[1,768,2048]{2,1,0:T(8,128)(2,1)S(1)}, bf16[1,768,2048]{2,1,0:T(8,128)(2,1)}, u32[]{:S(2)}) copy-start(bf16[1,768,2048]{2,1,0:T(8,128)(2,1)} %param.7) | copy-start | bytes 9437188
where the time goes:
time: 524 us; the launch traced here: 523 us
  waiting for transfers between devices  216 us (41%)
  other arithmetic  130 us (25%)
  local copies, waits for them, and re-layouts  106 us (20%)
  blocking collectives  35.5 us (7%)
  starting transfers between devices  22.8 us (4%)
  matrix products  12.2 us (2%)
    all_to_all x1, waiting for transfers between devices, local_step(): ret_buf = lax.all_to_all(back_buf, 'ep', 0, 0, tiled=True)  108 us
    all_to_all x1, waiting for transfers between devices, local_step(): recv_buf = lax.all_to_all(send_buf, 'ep', 0, 0, tiled=True)  108 us
    top_k x1, other arithmetic, local_step(): top_vals, top_ids = lax.top_k(logits, 2)  82.7 us
    all_gather x1, blocking collectives, local_step(): all_counts = lax.all_gather(local_counts, 'ep').astype(jnp.int32)  35.5 us
    gather x2, local copies, waits for them, and re-layouts, local_step(): rows_back = jnp.take(ret_buf, send_row, axis=0, mode='fill', fill_value=0)  20.9 us
    gather x1, local copies, waits for them, and re-layouts, local_step(): jnp.take(expert_out, back_row.reshape(-1), axis=0, mode='fill', fill_valu...  19.1 us
    reduce_sum x1, other arithmetic, local_step(): jnp.sum(pick_gate[:, :, None] * rows_back.astype(jnp.float32), axis=1)  19 us
    gather x1, local copies, waits for them, and re-layouts, local_step(): send_buf = jnp.take(x_rows, slot_tok, axis=0, mode='fill', fill_value=0)  18.2 us
  transfers between devices with their start and end apart: 2, of which 2 were waited for; matrix products, arithmetic and copies ran while one was open for 2% of the time, Pallas kernels for 0%

commit v1 on v0

v1 whole, which is shorter than its diff:
```python
import functools
import jax
import jax.numpy as jnp
from jax import lax
from jax.experimental import pallas as pl
from jax.experimental.pallas import tpu as pltpu
from jax.sharding import PartitionSpec as P

CAP_FACTOR = 2
F32, BF16 = jnp.float32, jnp.bfloat16
MESH = pl.DeviceIdType.MESH


def _grid_dims(n):
    return n // 32, 4, 4, 2


def _send_order(n):
    nz, ny, nx, nc = _grid_dims(n)
    hops = lambda a, m: min(a % m, m - a % m)
    dist = lambda o: hops(o[0], nz) + hops(o[1], ny) + hops(o[2], nx)
    todo = [(z, y, x, c) for z in range(nz) for y in range(ny) for x in range(nx) for c in range(nc)][1:]
    seen, order = set(), []
    for z, y, x, c in sorted(todo, key=lambda o: (-dist(o), o)):
        for a, b, d in ((z, y, x), (y, x, z), (x, z, y)):
            for s in (1, -1):
                q = (s * a % nz, s * b % ny, s * d % nx, c)
                if q not in seen and any(q):
                    seen.add(q)
                    order.append(q)
    assert sorted(order) == sorted(todo)
    return order


def _shift(me, n, offset, sign):
    nz, ny, nx, nc = _grid_dims(n)
    dz, dy, dx, dc = offset
    if sign < 0:
        dz, dy, dx = (nz - dz) % nz, (ny - dy) % ny, (nx - dx) % nx
    z, y, x, c = me // (ny * nx * nc), (me // (nx * nc)) % ny, (me // nc) % nx, me % nc
    return (((z + dz) % nz * ny + (y + dy) % ny) * nx + (x + dx) % nx) * nc + (c + dc) % nc


def _route_pack(src_cap, logits_ref, x_ref, send_ref, meta_ref, cnt_ref, slot_row):
    step = pl.program_id(0)

    @pl.when(step == 0)
    def _():
        lg = logits_ref[...]
        tok, experts = lg.shape
        lane = lax.broadcasted_iota(jnp.int32, lg.shape, 1)
        m1 = jnp.max(lg, axis=1, keepdims=True)
        i1 = jnp.min(jnp.where(lg == m1, lane, experts), axis=1, keepdims=True)
        rest = jnp.where(lane == i1, -jnp.inf, lg)
        m2 = jnp.max(rest, axis=1, keepdims=True)
        i2 = jnp.min(jnp.where(rest == m2, lane, experts), axis=1, keepdims=True)
        hot1, hot2 = lane == i1, lane == i2
        chosen = jnp.where(hot1 | hot2, 1.0, 0.0)
        total = jnp.sum(jnp.exp(lg - m1), axis=1, keepdims=True)
        g1 = 1.0 / total
        g2 = jnp.exp(m2 - m1) / total
        later = lax.broadcasted_iota(jnp.int32, (tok, tok), 0)
        early = lax.broadcasted_iota(jnp.int32, (tok, tok), 1)
        tri = jnp.where(early < later, 1.0, 0.0).astype(BF16)
        before = jnp.dot(tri, chosen.astype(BF16), preferred_element_type=F32)
        p1 = jnp.sum(jnp.where(hot1, before, 0.0), axis=1, keepdims=True)
        p2 = jnp.sum(jnp.where(hot2, before, 0.0), axis=1, keepdims=True)
        cnt_ref[...] = jnp.sum(chosen, axis=0, keepdims=True)
        e1, e2 = i1.astype(F32), i2.astype(F32)
        meta = jnp.where(lane == 0, g1, jnp.where(lane == 1, g2, jnp.where(lane == 2, e1, jnp.where(
            lane == 3, e2, jnp.where(lane == 4, p1, jnp.where(lane == 5, p2, jnp.where(
                lane == 6, e1 * src_cap + p1, jnp.where(lane == 7, e2 * src_cap + p2, 0.0))))))))
        meta_ref[...] = meta
        slot_row[...] = meta.T[0:8, :].astype(jnp.int32)

    rows = send_ref.shape[0]
    slot = lax.broadcasted_iota(jnp.int32, (rows, x_ref.shape[0]), 0) + step * rows
    pick = (slot == slot_row[6:7, :]) | (slot == slot_row[7:8, :])
    hot = jnp.where(pick, 1.0, 0.0).astype(BF16)
    send_ref[...] = jnp.dot(hot, x_ref[...], preferred_element_type=F32).astype(BF16)


def _exchange(n, group, send_ref, cnt_ref, w1_ref, w2_ref, ret_ref, all_ref, got_ref, rows_ref, z_ref,
              out_sem, got_sem, back_sem, ret_sem, cnt_out, cnt_got, own_sem, load_sem):
    me = lax.axis_index("ep")
    order = _send_order(n)
    cap = send_ref.shape[1]

    bar = pltpu.get_barrier_semaphore()

    def greet(k, carry):
        pl.semaphore_signal(bar, inc=1, device_id={"ep": (me + k) % n}, device_id_type=MESH)
        return carry

    lax.fori_loop(1, n, greet, 0)
    pl.semaphore_wait(bar, n - 1)

    def tell(k, carry):
        pltpu.make_async_remote_copy(cnt_ref, all_ref.at[me], cnt_out, cnt_got, device_id={"ep": (me + k) % n},
                                     device_id_type=MESH).start()
        return carry

    lax.fori_loop(1, n, tell, 0)
    for i, off in enumerate(order):
        peer = _shift(me, n, off, 1)
        pltpu.make_async_remote_copy(send_ref.at[peer], got_ref.at[i], out_sem, got_sem.at[i // group],
                                     device_id={"ep": peer}, device_id_type=MESH).start()
    own = pltpu.make_async_copy(send_ref.at[me], got_ref.at[n - 1], own_sem)
    own.start()
    own_cnt = pltpu.make_async_copy(cnt_ref, all_ref.at[me], own_sem)
    w1, w2 = w1_ref, w2_ref
    own.wait()
    own_cnt.start()
    own_cnt.wait()

    for g in range(n // group):
        lo = g * group
        cnt = min(group, n - 1 - lo)
        block = got_ref.at[pl.ds(lo, cnt)]
        pltpu.make_async_copy(block, block, got_sem.at[g]).wait()
        load = pltpu.make_async_copy(got_ref.at[pl.ds(lo, group)], rows_ref, load_sem)
        load.start()
        load.wait()
        x = rows_ref[...].reshape(group * cap, rows_ref.shape[2])
        h = jax.nn.gelu(jnp.dot(x, w1[...], preferred_element_type=F32), approximate=True).astype(BF16)
        z = jnp.dot(h, w2[...], preferred_element_type=F32).astype(BF16)
        z_ref[pl.ds(lo, group)] = z.reshape(group, cap, z.shape[1])
        for i in range(lo, lo + cnt):
            peer = _shift(me, n, order[i], -1)
            pltpu.make_async_remote_copy(z_ref.at[i], ret_ref.at[me], back_sem, ret_sem, device_id={"ep": peer},
                                         device_id_type=MESH).start()
    own_z = pltpu.make_async_copy(z_ref.at[n - 1], ret_ref.at[me], own_sem)
    own_z.start()
    own_z.wait()

    rest = pl.ds(0, n - 1)
    pltpu.make_async_copy(send_ref.at[rest], send_ref.at[rest], out_sem).wait()
    pltpu.make_async_copy(z_ref.at[rest], z_ref.at[rest], back_sem).wait()
    pltpu.make_async_copy(all_ref.at[rest], all_ref.at[rest], cnt_out).wait()
    pltpu.make_async_copy(all_ref.at[rest], all_ref.at[rest], cnt_got).wait()
    pltpu.make_async_copy(ret_ref.at[rest], ret_ref.at[rest], ret_sem).wait()


def _combine(capacity, src_cap, base_ref, ret_ref, x_ref, meta_ref, out_ref, pick1, pick2):
    @pl.when(pl.program_id(0) == 0)
    def _():
        meta = meta_ref[...]
        base = base_ref[...]
        lane = lax.broadcasted_iota(jnp.int32, meta.shape, 1).astype(F32)
        slots = lax.broadcasted_iota(jnp.int32, pick1.shape, 1).astype(F32)
        for c, pick in ((0, pick1), (1, pick2)):
            e, pos, slot = meta[:, 2 + c:3 + c], meta[:, 4 + c:5 + c], meta[:, 6 + c:7 + c]
            ahead = jnp.sum(jnp.where(lane == e, base, 0.0), axis=1, keepdims=True)
            slot = jnp.where(pos + ahead < capacity, slot, -1.0)
            pick[...] = jnp.where(slots == slot, 1.0, 0.0).astype(BF16)

    z = ret_ref[...]
    r1 = jnp.dot(pick1[...], z, preferred_element_type=F32)
    r2 = jnp.dot(pick2[...], z, preferred_element_type=F32)
    y = meta_ref[:, 0:1] * r1 + meta_ref[:, 1:2] * r2
    out_ref[...] = (x_ref[...].astype(F32) + y).astype(BF16)


def solution(mesh):
    n = mesh.shape["ep"]
    row_spec = P(("dp", "ep"), None)
    expert_spec = P("ep", None, None)

    def local_step(x_rows, logits, w_in, w_out):
        tok, d_model = x_rows.shape
        experts = logits.shape[1]
        ff = w_in.shape[2]
        capacity = CAP_FACTOR * tok * n // experts
        src_cap = 4 * tok // experts
        slots = experts * src_cap
        blk = 256
        whole = lambda *s: pl.BlockSpec(s, lambda i: (0,) * len(s))
        send, meta, cnt = pl.pallas_call(
            functools.partial(_route_pack, src_cap),
            grid=(slots // blk,),
            in_specs=[whole(tok, experts), whole(tok, d_model)],
            out_specs=[pl.BlockSpec((blk, d_model), lambda i: (i, 0)), whole(tok, experts), whole(1, experts)],
            out_shape=[jax.ShapeDtypeStruct((slots, d_model), BF16), jax.ShapeDtypeStruct((tok, experts), F32),
                       jax.ShapeDtypeStruct((1, experts), F32)],
            scratch_shapes=[pltpu.VMEM((8, tok), jnp.int32)],
            name="route_pack",
        )(logits, x_rows)

        group = 16
        any_ = pl.BlockSpec(memory_space=pl.ANY)
        vmem = pl.BlockSpec(memory_space=pltpu.VMEM)
        dma = pltpu.SemaphoreType.DMA
        ret, all_cnt, _ = pl.pallas_call(
            functools.partial(_exchange, n, group),
            in_specs=[any_, any_, vmem, vmem],
            out_specs=[any_, any_, any_],
            out_shape=[jax.ShapeDtypeStruct((n, src_cap, d_model), BF16), jax.ShapeDtypeStruct((n, 1, experts), F32),
                       jax.ShapeDtypeStruct((n, src_cap, d_model), BF16)],
            scratch_shapes=[pltpu.VMEM((group, src_cap, d_model), BF16), pltpu.VMEM((n, src_cap, d_model), BF16),
                            dma, dma((n // group,)), dma, dma, dma, dma, dma, dma],
            compiler_params=pltpu.CompilerParams(collective_id=0, has_side_effects=True, vmem_limit_bytes=60 * 2**20),
            name="exchange",
        )(send.reshape(n, src_cap, d_model), cnt, w_in[0], w_out[0])

        me = lax.axis_index("ep")
        ahead = (jnp.arange(n) < me).astype(F32)[:, None]
        base = jnp.sum(all_cnt[:, 0, :] * ahead, axis=0, keepdims=True)
        cols = 256
        return pl.pallas_call(
            functools.partial(_combine, capacity, src_cap),
            grid=(d_model // cols,),
            in_specs=[whole(1, experts), pl.BlockSpec((slots, cols), lambda i: (0, i)),
                      pl.BlockSpec((tok, cols), lambda i: (0, i)), whole(tok, experts)],
            out_specs=pl.BlockSpec((tok, cols), lambda i: (0, i)),
            out_shape=jax.ShapeDtypeStruct((tok, d_model), BF16),
            scratch_shapes=[pltpu.VMEM((tok, slots), BF16), pltpu.VMEM((tok, slots), BF16)],
            name="combine",
        )(base, ret.reshape(slots, d_model), x_rows, meta)

    return jax.shard_map(local_step, mesh=mesh, in_specs=(row_spec, row_spec, expert_spec, expert_spec),
                         out_specs=row_spec, check_vma=False)
```

time: 524 us -> 289 us (0.55)
  the two profiles are of different devices: /device:TPU:12 before, /device:TPU:1 now
where the time goes in v1:
time: 289 us
  Pallas kernels  287 us (99%)
    pallas_call x1, Pallas kernels, local_step(): pl.pallas_call(functools.partial(_exchange, n, group), in_specs=[any_, an...  263 us
    pallas_call x1, Pallas kernels, local_step(): pl.pallas_call(functools.partial(_combine, capacity, src_cap), grid=(d_mo...  13.8 us
    pallas_call x1, Pallas kernels, local_step(): pl.pallas_call(functools.partial(_route_pack, src_cap), grid=(slots // bl...  10.6 us

profile of v1, /device:TPU:1, one launch (start us, length us, event | category | flops | bytes accessed | tf_op | source)
XLA Modules:
  0.0 288.5 jit_solution(10807502948858870657)
XLA Ops:
  0.0 10.6 %route_pack.1 = (bf16[2048,2048]{1,0:T(8,128)(2,1)}, f32[512,128]{1,0:T(8,128)}, f32[1,128]{1,0:T(1,128)}) custom-call(f32[512,128]{1,0:T(8,128)} %logits_ref.1, bf16[512,2048]{1,0:T(8,128)(2,1)} %x_ref.3), custom_call_target="tpu_custom_call" | custom-call | tf_op jit(solution)/shard_map/route_pack/pallas_call | solution.py:178
  10.6 262.7 %exchange.1 = (bf16[128,16,2048]{2,1,0:T(8,128)(2,1)}, f32[128,1,128]{2,1,0:T(1,128)}, bf16[128,16,2048]{2,1,0:T(8,128)(2,1)}) custom-call(bf16[128,16,2048]{2,1,0:T(8,128)(2,1)} %bitcast.7, f32[1,128]{1,0:T(1,128)} %get-tuple-element.11.cnt_ref, bf16[2048,768]{1,0:T(8,128)(2,1)} %bitcast.8, bf16[768,2048]{1,0:T(8,128)(2,1)} %bitcast.9), custom_call_target="tpu_custom_call" | custom-call | tf_op jit(solution)/shard_map/exchange/pallas_call | solution.py:193
  273.3 1.4 multiply_reduce_fusion
  274.7 13.8 %combine.1 = bf16[512,2048]{1,0:T(8,128)(2,1)} custom-call(f32[1,128]{1,0:T(1,128)} %bitcast.11, bf16[2048,2048]{1,0:T(8,128)(2,1)} %bitcast.6, bf16[512,2048]{1,0:T(8,128)(2,1)} %x_ref.3, f32[512,128]{1,0:T(8,128)} %get-tuple-element.14.meta_ref), custom_call_target="tpu_custom_call" | custom-call | tf_op jit(solution)/shard_map/combine/pallas_call | solution.py:209
  (1 shorter events, 0.0 us)

commit v2 on v1

--- a/solution.py
+++ b/solution.py
@@ -9,6 +9,7 @@
 CAP_FACTOR = 2
 F32, BF16 = jnp.float32, jnp.bfloat16
 MESH = pl.DeviceIdType.MESH
+BF16_MAX = float(jnp.finfo(jnp.bfloat16).max)
 
 
 def _grid_dims(n):
@@ -80,11 +81,12 @@
     send_ref[...] = jnp.dot(hot, x_ref[...], preferred_element_type=F32).astype(BF16)
 
 
-def _exchange(n, group, send_ref, cnt_ref, w1_ref, w2_ref, ret_ref, all_ref, got_ref, rows_ref, z_ref,
-              out_sem, got_sem, back_sem, ret_sem, cnt_out, cnt_got, own_sem, load_sem):
+def _exchange(n, group, send_ref, cnt_ref, w1_ref, w2_ref, ret_ref, all_ref, got_ref, zh_ref, rows, zv,
+              out_sem, got_sem, back_sem, ret_sem, cnt_out, cnt_got, own_sem, load_sem, store_sem):
     me = lax.axis_index("ep")
     order = _send_order(n)
-    cap = send_ref.shape[1]
+    cap, d_model = send_ref.shape[1:]
+    chunks = n // group
 
     bar = pltpu.get_barrier_semaphore()
 
@@ -94,6 +96,15 @@
 
     lax.fori_loop(1, n, greet, 0)
     pl.semaphore_wait(bar, n - 1)
+
+    def span(j):
+        return range(j * group, min((j + 1) * group, n - 1))
+
+    for j in range(chunks):
+        for i in span(j):
+            peer = _shift(me, n, order[i], 1)
+            pltpu.make_async_remote_copy(send_ref.at[peer], got_ref.at[i], out_sem, got_sem.at[j],
+                                         device_id={"ep": peer}, device_id_type=MESH).start()
 
     def tell(k, carry):
         pltpu.make_async_remote_copy(cnt_ref, all_ref.at[me], cnt_out, cnt_got, device_id={"ep": (me + k) % n},
@@ -101,63 +112,68 @@
         return carry
 
     lax.fori_loop(1, n, tell, 0)
-    for i, off in enumerate(order):
-        peer = _shift(me, n, off, 1)
-        pltpu.make_async_remote_copy(send_ref.at[peer], got_ref.at[i], out_sem, got_sem.at[i // group],
-                                     device_id={"ep": peer}, device_id_type=MESH).start()
     own = pltpu.make_async_copy(send_ref.at[me], got_ref.at[n - 1], own_sem)
     own.start()
+    own.wait()
     own_cnt = pltpu.make_async_copy(cnt_ref, all_ref.at[me], own_sem)
-    w1, w2 = w1_ref, w2_ref
-    own.wait()
     own_cnt.start()
     own_cnt.wait()
 
-    for g in range(n // group):
-        lo = g * group
-        cnt = min(group, n - 1 - lo)
-        block = got_ref.at[pl.ds(lo, cnt)]
-        pltpu.make_async_copy(block, block, got_sem.at[g]).wait()
-        load = pltpu.make_async_copy(got_ref.at[pl.ds(lo, group)], rows_ref, load_sem)
+    def z_store(j):
+        return pltpu.make_async_copy(zv.at[j % 2], zh_ref.at[pl.ds(j * group, group)], store_sem.at[j % 2])
+
+    def back(j):
+        z_store(j).wait()
+        for i in span(j):
+            pltpu.make_async_remote_copy(zh_ref.at[i], ret_ref.at[me], back_sem, ret_sem,
+                                         device_id={"ep": _shift(me, n, order[i], -1)}, device_id_type=MESH).start()
+
+    for j in range(chunks):
+        block = got_ref.at[pl.ds(j * group, len(span(j)))]
+        pltpu.make_async_copy(block, block, got_sem.at[j]).wait()
+        load = pltpu.make_async_copy(got_ref.at[pl.ds(j * group, group)], rows, load_sem)
         load.start()
+        if j > 0:
+            back(j - 1)
         load.wait()
-        x = rows_ref[...].reshape(group * cap, rows_ref.shape[2])
-        h = jax.nn.gelu(jnp.dot(x, w1[...], preferred_element_type=F32), approximate=True).astype(BF16)
-        z = jnp.dot(h, w2[...], preferred_element_type=F32).astype(BF16)
-        z_ref[pl.ds(lo, group)] = z.reshape(group, cap, z.shape[1])
-        for i in range(lo, lo + cnt):
-            peer = _shift(me, n, order[i], -1)
-            pltpu.make_async_remote_copy(z_ref.at[i], ret_ref.at[me], back_sem, ret_sem, device_id={"ep": peer},
-                                         device_id_type=MESH).start()
-    own_z = pltpu.make_async_copy(z_ref.at[n - 1], ret_ref.at[me], own_sem)
+        xs = rows[...].reshape(group * cap, d_model)
+        h = jax.nn.gelu(jnp.dot(xs, w1_ref[...], preferred_element_type=F32), approximate=True).astype(BF16)
+        z = jnp.dot(h, w2_ref[...], preferred_element_type=F32)
+        z = jnp.clip(z, -BF16_MAX, BF16_MAX)
+        zv[j % 2] = z.astype(BF16).reshape(group, cap, d_model)
+        z_store(j).start()
+    back(chunks - 1)
+    own_z = pltpu.make_async_copy(zv.at[(chunks - 1) % 2, group - 1], ret_ref.at[me], own_sem)
     own_z.start()
     own_z.wait()
 
     rest = pl.ds(0, n - 1)
     pltpu.make_async_copy(send_ref.at[rest], send_ref.at[rest], out_sem).wait()
-    pltpu.make_async_copy(z_ref.at[rest], z_ref.at[rest], back_sem).wait()
+    pltpu.make_async_copy(zh_ref.at[rest], zh_ref.at[rest], back_sem).wait()
     pltpu.make_async_copy(all_ref.at[rest], all_ref.at[rest], cnt_out).wait()
     pltpu.make_async_copy(all_ref.at[rest], all_ref.at[rest], cnt_got).wait()
     pltpu.make_async_copy(ret_ref.at[rest], ret_ref.at[rest], ret_sem).wait()
 
 
-def _combine(capacity, src_cap, base_ref, ret_ref, x_ref, meta_ref, out_ref, pick1, pick2):
+def _combine(capacity, base_ref, ret_ref, x_ref, meta_ref, out_ref, pick):
+    tok = x_ref.shape[0]
+
     @pl.when(pl.program_id(0) == 0)
     def _():
         meta = meta_ref[...]
         base = base_ref[...]
         lane = lax.broadcasted_iota(jnp.int32, meta.shape, 1).astype(F32)
-        slots = lax.broadcasted_iota(jnp.int32, pick1.shape, 1).astype(F32)
-        for c, pick in ((0, pick1), (1, pick2)):
+        slots = lax.broadcasted_iota(jnp.int32, (tok, pick.shape[1]), 1).astype(F32)
+        for c in range(2):
             e, pos, slot = meta[:, 2 + c:3 + c], meta[:, 4 + c:5 + c], meta[:, 6 + c:7 + c]
             ahead = jnp.sum(jnp.where(lane == e, base, 0.0), axis=1, keepdims=True)
             slot = jnp.where(pos + ahead < capacity, slot, -1.0)
-            pick[...] = jnp.where(slots == slot, 1.0, 0.0).astype(BF16)
+            pick[c * tok:(c + 1) * tok, :] = jnp.where(slots == slot, 1.0, 0.0).astype(BF16)
 
     z = ret_ref[...]
-    r1 = jnp.dot(pick1[...], z, preferred_element_type=F32)
-    r2 = jnp.dot(pick2[...], z, preferred_element_type=F32)
-    y = meta_ref[:, 0:1] * r1 + meta_ref[:, 1:2] * r2
+    z = jnp.where(z == z, z, jnp.zeros_like(z))
+    r = jnp.dot(pick[...], z, preferred_element_type=F32)
+    y = meta_ref[:, 0:1] * r[0:tok] + meta_ref[:, 1:2] * r[tok:2 * tok]
     out_ref[...] = (x_ref[...].astype(F32) + y).astype(BF16)
 
 
@@ -190,14 +206,15 @@
         any_ = pl.BlockSpec(memory_space=pl.ANY)
         vmem = pl.BlockSpec(memory_space=pltpu.VMEM)
         dma = pltpu.SemaphoreType.DMA
-        ret, all_cnt, _ = pl.pallas_call(
+        ret, all_cnt, _, _ = pl.pallas_call(
             functools.partial(_exchange, n, group),
             in_specs=[any_, any_, vmem, vmem],
-            out_specs=[any_, any_, any_],
+            out_specs=[any_, any_, any_, any_],
             out_shape=[jax.ShapeDtypeStruct((n, src_cap, d_model), BF16), jax.ShapeDtypeStruct((n, 1, experts), F32),
+                       jax.ShapeDtypeStruct((n, src_cap, d_model), BF16),
                        jax.ShapeDtypeStruct((n, src_cap, d_model), BF16)],
-            scratch_shapes=[pltpu.VMEM((group, src_cap, d_model), BF16), pltpu.VMEM((n, src_cap, d_model), BF16),
-                            dma, dma((n // group,)), dma, dma, dma, dma, dma, dma],
+            scratch_shapes=[pltpu.VMEM((group, src_cap, d_model), BF16), pltpu.VMEM((2, group, src_cap, d_model), BF16),
+                            dma, dma((n // group,)), dma, dma, dma, dma, dma, dma, dma((2,))],
             compiler_params=pltpu.CompilerParams(collective_id=0, has_side_effects=True, vmem_limit_bytes=60 * 2**20),
             name="exchange",
         )(send.reshape(n, src_cap, d_model), cnt, w_in[0], w_out[0])
@@ -207,13 +224,13 @@
         base = jnp.sum(all_cnt[:, 0, :] * ahead, axis=0, keepdims=True)
         cols = 256
         return pl.pallas_call(
-            functools.partial(_combine, capacity, src_cap),
+            functools.partial(_combine, capacity),
             grid=(d_model // cols,),
             in_specs=[whole(1, experts), pl.BlockSpec((slots, cols), lambda i: (0, i)),
                       pl.BlockSpec((tok, cols), lambda i: (0, i)), whole(tok, experts)],
             out_specs=pl.BlockSpec((tok, cols), lambda i: (0, i)),
             out_shape=jax.ShapeDtypeStruct((tok, d_model), BF16),
-            scratch_shapes=[pltpu.VMEM((tok, slots), BF16), pltpu.VMEM((tok, slots), BF16)],
+            scratch_shapes=[pltpu.VMEM((2 * tok, slots), BF16)],
             name="combine",
         )(base, ret.reshape(slots, d_model), x_rows, meta)
 

time: 289 us -> 269 us (0.931)
  the two profiles are of different devices: /device:TPU:1 before, /device:TPU:16 now
where the time goes in v2:
time: 269 us
  Pallas kernels  267 us (99%)
    pallas_call x1, Pallas kernels, local_step(): pl.pallas_call(functools.partial(_exchange, n, group), in_specs=[any_, an...  243 us
    pallas_call x1, Pallas kernels, local_step(): pl.pallas_call(functools.partial(_combine, capacity), grid=(d_model // co...  13.8 us
    pallas_call x1, Pallas kernels, local_step(): pl.pallas_call(functools.partial(_route_pack, src_cap), grid=(slots // bl...  10.7 us

profile of v2, /device:TPU:16, one launch (start us, length us, event | category | flops | bytes accessed | tf_op | source)
XLA Modules:
  0.0 268.7 jit_solution(2475104853233587545)
XLA Ops:
  0.0 10.7 %route_pack.1 = (bf16[2048,2048]{1,0:T(8,128)(2,1)}, f32[512,128]{1,0:T(8,128)}, f32[1,128]{1,0:T(1,128)}) custom-call(f32[512,128]{1,0:T(8,128)} %logits_ref.1, bf16[512,2048]{1,0:T(8,128)(2,1)} %x_ref.3), custom_call_target="tpu_custom_call" | custom-call | tf_op jit(solution)/shard_map/route_pack/pallas_call | solution.py:194
  10.7 242.8 %exchange.1 = (bf16[128,16,2048]{2,1,0:T(8,128)(2,1)}, f32[128,1,128]{2,1,0:T(1,128)}, bf16[128,16,2048]{2,1,0:T(8,128)(2,1)}, bf16[128,16,2048]{2,1,0:T(8,128)(2,1)}) custom-call(bf16[128,16,2048]{2,1,0:T(8,128)(2,1)} %bitcast.7, f32[1,128]{1,0:T(1,128)} %get-tuple-element.11.cnt_ref, bf16[2048,768]{1,0:T(8,128)(2,1)} %bitcast.8, bf16[768,2048]{1,0:T(8,128)(2,1)} %bitcast.9), custom_call_target="tpu_custom_call" | custom-call | tf_op jit(solution)/shard_map/exchange/pallas_call | solution.py:209
  253.5 1.4 multiply_reduce_fusion
  254.9 13.8 %combine.1 = bf16[512,2048]{1,0:T(8,128)(2,1)} custom-call(f32[1,128]{1,0:T(1,128)} %bitcast.11, bf16[2048,2048]{1,0:T(8,128)(2,1)} %bitcast.6, bf16[512,2048]{1,0:T(8,128)(2,1)} %x_ref.3, f32[512,128]{1,0:T(8,128)} %get-tuple-element.14.meta_ref), custom_call_target="tpu_custom_call" | custom-call | tf_op jit(solution)/shard_map/combine/pallas_call | solution.py:226
  (1 shorter events, 0.0 us)

commit v3 on v2

v3 whole, which is shorter than its diff:
```python
import functools
import jax
import jax.numpy as jnp
import numpy as np
from jax import lax
from jax.experimental import pallas as pl
from jax.experimental.pallas import tpu as pltpu
from jax.sharding import PartitionSpec as P

CAP_FACTOR = 2
F32, BF16, I32 = jnp.float32, jnp.bfloat16, jnp.int32
MESH = pl.DeviceIdType.MESH
BF16_MAX = float(jnp.finfo(jnp.bfloat16).max)
SIDE, CORES = 4, 2


def _send_order(chips):
    nz = chips // SIDE**2
    hops = lambda a, m: min(a % m, m - a % m)
    dist = lambda o: hops(o[0], nz) + hops(o[1], SIDE) + hops(o[2], SIDE)
    todo = [(z, y, x) for z in range(nz) for y in range(SIDE) for x in range(SIDE)][1:]
    seen, order = set(), []
    for z, y, x in sorted(todo, key=lambda o: (-dist(o), o)):
        for a, b, d in ((z, y, x), (y, x, z), (x, z, y)):
            for s in (1, -1):
                q = (s * a % nz, s * b % SIDE, s * d % SIDE)
                if q not in seen and any(q):
                    seen.add(q)
                    order.append(q)
    assert sorted(order) == sorted(todo)
    return order + [(0, 0, 0)]


def _chip_at(chip, chips, dz, dy, dx):
    nz = chips // SIDE**2
    z, y, x = chip // SIDE**2, (chip // SIDE) % SIDE, chip % SIDE
    return ((z + dz) % nz * SIDE + (y + dy) % SIDE) * SIDE + (x + dx) % SIDE


def _route_pack(n, cap, logits_ref, x_ref, off_ref, send_ref, hot_ref, meta_ref, cnt_ref):
    step = pl.program_id(0)
    tok, experts = logits_ref.shape

    @pl.when(step == 0)
    def _():
        lg = logits_ref[...]
        lane = lax.broadcasted_iota(I32, lg.shape, 1)
        m1 = jnp.max(lg, axis=1, keepdims=True)
        i1 = jnp.min(jnp.where(lg == m1, lane, experts), axis=1, keepdims=True)
        rest = jnp.where(lane == i1, -jnp.inf, lg)
        m2 = jnp.max(rest, axis=1, keepdims=True)
        i2 = jnp.min(jnp.where(rest == m2, lane, experts), axis=1, keepdims=True)
        hot1, hot2 = lane == i1, lane == i2
        chosen = jnp.where(hot1 | hot2, 1.0, 0.0)
        total = jnp.sum(jnp.exp(lg - m1), axis=1, keepdims=True)
        later = lax.broadcasted_iota(I32, (tok, tok), 0)
        early = lax.broadcasted_iota(I32, (tok, tok), 1)
        tri = jnp.where(early < later, 1.0, 0.0).astype(BF16)
        before = jnp.dot(tri, chosen.astype(BF16), preferred_element_type=F32)
        p1 = jnp.sum(jnp.where(hot1, before, 0.0), axis=1, keepdims=True)
        p2 = jnp.sum(jnp.where(hot2, before, 0.0), axis=1, keepdims=True)
        e1, e2 = i1.astype(F32), i2.astype(F32)
        cnt_ref[...] = jnp.sum(chosen, axis=0, keepdims=True)
        table = jnp.zeros_like(lg)
        for k, col in enumerate((1.0 / total, jnp.exp(m2 - m1) / total, e1, e2, p1, p2, e1 * cap + p1, e2 * cap + p2)):
            table = jnp.where(lane == k, col, table)
        meta_ref[...] = table

    off = off_ref[pl.ds(step, 1)].reshape(1, send_ref.shape[0])
    chip = lax.axis_index("ep") // CORES
    z, y, x = chip // SIDE**2, (chip // SIDE) % SIDE, chip % SIDE
    chips = n // CORES
    nz = chips // SIDE**2
    dz, dy, dx = off // SIDE**2, (off // SIDE) % SIDE, off % SIDE
    other = ((z + dz) % nz * SIDE + (y + dy) % SIDE) * SIDE + (x + dx) % SIDE
    place = lax.broadcasted_iota(I32, off.shape, 1) % (CORES * cap)
    slot = (other * (CORES * cap) + place).astype(F32)
    first = jnp.where(meta_ref[:, 6:7] == slot, 1.0, 0.0)
    second = jnp.where(meta_ref[:, 7:8] == slot, 1.0, 0.0)
    hot_ref[0:tok, :] = first.astype(BF16)
    hot_ref[tok:2 * tok, :] = second.astype(BF16)
    send_ref[...] = lax.dot_general((first + second).astype(BF16), x_ref[...], (((0,), (0,)), ((), ())),
                                    preferred_element_type=F32).astype(BF16)


def _exchange(n, group, send_ref, cnt_ref, hot_hbm, w1_ref, w2_ref, picked_ref, all_ref, got_ref, side_ref, zp_ref, ret_ref,
              rows, zv, hot, out_sem, got_sem, fw_out, fw_got, z_out, z_got, back_sem, ret_sem, cnt_out, cnt_got,
              own_sem, load_sem, store_sem):
    me = lax.axis_index("ep")
    chips = n // CORES
    chip, core = me // CORES, me % CORES
    sibling = chip * CORES + 1 - core
    order = _send_order(chips)
    cap, d_model = send_ref.shape[1:]
    half = group // CORES
    chunks = chips // half

    bar = pltpu.get_barrier_semaphore()

    def greet(k, carry):
        pl.semaphore_signal(bar, inc=1, device_id={"ep": (me + k) % n}, device_id_type=MESH)
        return carry

    lax.fori_loop(1, n, greet, 0)
    pl.semaphore_wait(bar, n - 1)

    def span(j):
        return range(j * half, min((j + 1) * half, chips - 1))

    def remote(src, dst, out, got, to):
        return pltpu.make_async_remote_copy(src, dst, out, got, device_id={"ep": to}, device_id_type=MESH)

    def pair(i):
        return pl.ds(i * CORES, CORES)

    for j in range(chunks):
        for i in span(j):
            to = _chip_at(chip, chips, *order[i]) * CORES + core
            remote(send_ref.at[pair(i)], got_ref.at[i], out_sem, got_sem.at[j], to).start()

    def tell(k, carry):
        remote(cnt_ref, all_ref.at[me], cnt_out, cnt_got, (me + k) % n).start()
        return carry

    lax.fori_loop(1, n, tell, 0)
    own = pltpu.make_async_copy(send_ref.at[pair(chips - 1)], got_ref.at[chips - 1], own_sem)
    own.start()
    own.wait()
    own_cnt = pltpu.make_async_copy(cnt_ref, all_ref.at[me], own_sem)
    own_cnt.start()
    own_cnt.wait()

    def some(j):
        return pl.ds(j * half, half)

    def hand(j):
        return remote(got_ref.at[some(j), 1 - core], side_ref.at[some(j)], fw_out, fw_got.at[j], sibling)

    def z_store(j):
        return pltpu.make_async_copy(zv.at[j % 2, pl.ds(0, half)], zp_ref.at[some(j), core], store_sem.at[j % 2])

    def z_hand(j):
        return remote(zv.at[j % 2, pl.ds(half, half)], zp_ref.at[some(j), core], z_out.at[j % 2], z_got.at[j], sibling)

    def back(j):
        z_store(j).wait()
        z_hand(j).wait_send()
        z_hand(j).wait_recv()
        for i in span(j):
            dz, dy, dx = order[i]
            to = _chip_at(chip, chips, chips // SIDE**2 - dz, SIDE - dy, SIDE - dx) * CORES + core
            remote(zp_ref.at[i], ret_ref.at[pair(i)], back_sem, ret_sem.at[j], to).start()

    for j in range(chunks + 1):
        if j < chunks:
            block = got_ref.at[pl.ds(j * half, len(span(j)))]
            pltpu.make_async_copy(block, block, got_sem.at[j]).wait()
            hand(j).start()
        if j == 0:
            continue
        p = j - 1
        direct = pltpu.make_async_copy(got_ref.at[some(p), core], rows.at[pl.ds(0, half)], load_sem.at[0])
        direct.start()
        hand(p).wait_recv()
        handed = pltpu.make_async_copy(side_ref.at[some(p)], rows.at[pl.ds(half, half)], load_sem.at[1])
        handed.start()
        if p > 0:
            back(p - 1)
        direct.wait()
        handed.wait()
        xs = rows[...].reshape(group * cap, d_model)
        h = jax.nn.gelu(jnp.dot(xs, w1_ref[...], preferred_element_type=F32), approximate=True).astype(BF16)
        z = jnp.dot(h, w2_ref[...], preferred_element_type=F32)
        z = jnp.clip(z, -BF16_MAX, BF16_MAX)
        zv[p % 2] = z.astype(BF16).reshape(group, cap, d_model)
        z_store(p).start()
        z_hand(p).start()
    back(chunks - 1)
    own_z = pltpu.make_async_copy(zp_ref.at[chips - 1], ret_ref.at[pair(chips - 1)], own_sem)
    own_z.start()
    own_z.wait()

    for j in range(chunks):
        lo = j * group
        block = ret_ref.at[pl.ds(lo, len(span(j)) * CORES)]
        get_hot = pltpu.make_async_copy(hot_hbm.at[j], hot, load_sem.at[1])
        get_hot.start()
        pltpu.make_async_copy(block, block, ret_sem.at[j]).wait()
        load = pltpu.make_async_copy(ret_ref.at[pl.ds(lo, group)], rows, load_sem.at[0])
        load.start()
        get_hot.wait()
        load.wait()
        part = jnp.dot(hot[...], rows[...].reshape(group * cap, d_model), preferred_element_type=F32).astype(BF16)
        picked_ref[...] = part if j == 0 else picked_ref[...] + part

    most = pl.ds(0, (chips - 1) * CORES)
    rest = pl.ds(0, n - 1)
    pltpu.make_async_copy(send_ref.at[most], send_ref.at[most], out_sem).wait()
    pltpu.make_async_copy(side_ref, side_ref, fw_out).wait()
    pltpu.make_async_copy(ret_ref.at[most], ret_ref.at[most], back_sem).wait()
    pltpu.make_async_copy(all_ref.at[rest], all_ref.at[rest], cnt_out).wait()
    pltpu.make_async_copy(all_ref.at[rest], all_ref.at[rest], cnt_got).wait()


def _finish(capacity, all_ref, x_ref, meta_ref, one_ref, two_ref, out_ref):
    me = lax.axis_index("ep")
    early = lax.broadcasted_iota(I32, all_ref.shape, 0) < me
    base = jnp.sum(jnp.where(early, all_ref[...], 0.0), axis=0)
    meta = meta_ref[...]
    lane = lax.broadcasted_iota(I32, meta.shape, 1).astype(F32)
    y = 0.0
    for k, z_ref in enumerate((one_ref, two_ref)):
        e, pos = meta[:, 2 + k:3 + k], meta[:, 4 + k:5 + k]
        before = pos + jnp.sum(jnp.where(lane == e, base, 0.0), axis=1, keepdims=True)
        y += jnp.where(before < capacity, meta[:, k:k + 1], 0.0) * z_ref[...].astype(F32)
    out_ref[...] = (x_ref[...].astype(F32) + y).astype(BF16)


def solution(mesh):
    n = mesh.shape["ep"]
    row_spec = P(("dp", "ep"), None)
    expert_spec = P("ep", None, None)

    def local_step(x_rows, logits, w_in, w_out):
        tok, d_model = x_rows.shape
        experts = logits.shape[1]
        capacity = CAP_FACTOR * tok * n // experts
        cap = 4 * tok // experts
        group = 16
        chips, chunks, width = n // CORES, n // group, group * cap
        code = np.array([(z * SIDE + y) * SIDE + x for z, y, x in _send_order(chips)], np.int32)
        offsets = jnp.asarray(np.repeat(code, CORES * cap).reshape(chunks, 1, width))
        whole = lambda *s: pl.BlockSpec(s, lambda i: (0,) * len(s))
        send, hot, meta, cnt = pl.pallas_call(
            functools.partial(_route_pack, n, cap),
            grid=(chunks,),
            in_specs=[whole(tok, experts), whole(tok, d_model), whole(chunks, 1, width)],
            out_specs=[pl.BlockSpec((width, d_model), lambda i: (i, 0)), pl.BlockSpec((2 * tok, width), lambda i: (i, 0)),
                       whole(tok, experts), whole(1, experts)],
            out_shape=[jax.ShapeDtypeStruct((chunks * width, d_model), BF16),
                       jax.ShapeDtypeStruct((chunks * 2 * tok, width), BF16),
                       jax.ShapeDtypeStruct((tok, experts), F32), jax.ShapeDtypeStruct((1, experts), F32)],
            name="route_pack",
        )(logits, x_rows, offsets)

        any_ = pl.BlockSpec(memory_space=pl.ANY)
        vmem = pl.BlockSpec(memory_space=pltpu.VMEM)
        dma = pltpu.SemaphoreType.DMA
        pairs = jax.ShapeDtypeStruct((chips, CORES, cap, d_model), BF16)
        picked, all_cnt = pl.pallas_call(
            functools.partial(_exchange, n, group),
            in_specs=[any_, any_, any_, vmem, vmem],
            out_specs=[vmem, any_, any_, any_, any_, any_],
            out_shape=[jax.ShapeDtypeStruct((2 * tok, d_model), BF16), jax.ShapeDtypeStruct((n, 1, experts), F32),
                       pairs, jax.ShapeDtypeStruct((chips, cap, d_model), BF16), pairs,
                       jax.ShapeDtypeStruct((n, cap, d_model), BF16)],
            scratch_shapes=[pltpu.VMEM((group, cap, d_model), BF16), pltpu.VMEM((2, group, cap, d_model), BF16),
                            pltpu.VMEM((2 * tok, width), BF16),
                            dma, dma((chunks,)), dma, dma((chunks,)), dma((2,)), dma((chunks,)), dma, dma((chunks,)),
                            dma, dma, dma, dma((2,)), dma((2,))],
            compiler_params=pltpu.CompilerParams(collective_id=0, has_side_effects=True, vmem_limit_bytes=60 * 2**20),
            name="exchange",
        )(send.reshape(n, cap, d_model), cnt, hot.reshape(chunks, 2 * tok, width), w_in[0], w_out[0])[:2]

        blk = tok // 4
        part = lambda s: pl.BlockSpec((blk, d_model), lambda i: (i + s, 0))
        return pl.pallas_call(
            functools.partial(_finish, capacity),
            grid=(tok // blk,),
            in_specs=[whole(n, 1, experts), part(0), pl.BlockSpec((blk, experts), lambda i: (i, 0)), part(0),
                      part(tok // blk)],
            out_specs=part(0),
            out_shape=jax.ShapeDtypeStruct((tok, d_model), BF16),
            name="finish",
        )(all_cnt, x_rows, meta, picked, picked)

    return jax.shard_map(local_step, mesh=mesh, in_specs=(row_spec, row_spec, expert_spec, expert_spec),
                         out_specs=row_spec, check_vma=False)
```

time: 269 us -> 276 us (1.026)
  the two profiles are of different devices: /device:TPU:16 before, /device:TPU:4 now
where the time goes in v3:
time: 276 us; the launch traced here: 275 us
  Pallas kernels  275 us (100%)
    pallas_call x1, Pallas kernels, local_step(): pl.pallas_call(functools.partial(_exchange, n, group), in_specs=[any_, an...  257 us
    pallas_call x1, Pallas kernels, local_step(): pl.pallas_call(functools.partial(_route_pack, n, cap), grid=(chunks,), in...  12 us
    pallas_call x1, Pallas kernels, local_step(): pl.pallas_call(functools.partial(_finish, capacity), grid=(tok // blk,),...  5.93 us

profile of v3, /device:TPU:4, one launch (start us, length us, event | category | flops | bytes accessed | tf_op | source)
XLA Modules:
  0.0 275.0 jit_solution(4527720913551566015)
XLA Ops:
  0.0 12.0 %route_pack.1 = (bf16[2048,2048]{1,0:T(8,128)(2,1)}, bf16[8192,256]{1,0:T(8,128)(2,1)}, f32[512,128]{1,0:T(8,128)}, f32[1,128]{1,0:T(1,128)}) custom-call(f32[512,128]{1,0:T(8,128)} %logits_ref.1, bf16[512,2048]{1,0:T(8,128)(2,1)} %x_ref.3, s32[8,1,256]{2,1,0:T(1,128)} %constant.2.clone.off_ref), custom_call_target="tpu_custom_call" | custom-call | tf_op jit(solution)/shard_map/route_pack/pallas_call | solution.py:234
  12.0 257.1 %exchange.1 = (bf16[1024,2048]{1,0:T(8,128)(2,1)}, f32[128,1,128]{2,1,0:T(1,128)}, bf16[64,2,16,2048]{3,2,1,0:T(8,128)(2,1)}, bf16[64,16,2048]{2,1,0:T(8,128)(2,...) custom-call(bf16[128,16,2048]{2,1,0:T(8,128)(2,1)} %bitcast.4, ...), custom_call_target="tpu_custom_call" | custom-call | tf_op jit(solution)/shard_map/exchange/pallas_call | solution.py:250
  269.1 5.9 %finish.1 = bf16[512,2048]{1,0:T(8,128)(2,1)} custom-call(f32[128,1,128]{2,1,0:T(1,128)} %get-tuple-element.14.all_ref, bf16[512,2048]{1,0:T(8,128)(2,1)} %x_ref.3, f32[512,128]{1,0:T(8,128)} %get-tuple-element.15.meta_ref, bf16[1024,2048]{1,0:T(8,128)(2,1)} %get-tuple-element.16.one_ref.two_ref, bf16[1024,2048]{1,0:T(8,128)(2,1)} %get-tuple-element.16.one_ref.two_ref), custom_call_target="tpu_custom_call" | custom-call | tf_op jit(solution)/shard_map/finish/pallas_call | solution.py:267

commit v4 on v3

v4 whole, which is shorter than its diff:
```python
import functools
import jax
import jax.numpy as jnp
import numpy as np
from jax import lax
from jax.experimental import pallas as pl
from jax.experimental.pallas import tpu as pltpu
from jax.sharding import PartitionSpec as P

CAP_FACTOR = 2
F32, BF16, I32 = jnp.float32, jnp.bfloat16, jnp.int32
MESH = pl.DeviceIdType.MESH
BF16_MAX = float(jnp.finfo(jnp.bfloat16).max)
SIDE, CORES = 4, 2


def _send_order(n):
    nz = n // (SIDE * SIDE * CORES)
    hops = lambda a, m: min(a % m, m - a % m)
    dist = lambda o: hops(o[0], nz) + hops(o[1], SIDE) + hops(o[2], SIDE)
    todo = [(z, y, x, c) for z in range(nz) for y in range(SIDE) for x in range(SIDE) for c in range(CORES)][1:]
    seen, order = set(), []
    for z, y, x, c in sorted(todo, key=lambda o: (-dist(o), o)):
        for a, b, d in ((z, y, x), (y, x, z), (x, z, y)):
            for s in (1, -1):
                q = (s * a % nz, s * b % SIDE, s * d % SIDE, c)
                if q not in seen and any(q):
                    seen.add(q)
                    order.append(q)
    assert sorted(order) == sorted(todo)
    return order + [(0, 0, 0, 0)]


def _device_at(me, n, dz, dy, dx, dc):
    nz = n // (SIDE * SIDE * CORES)
    z, y, x, c = me // (SIDE * SIDE * CORES), me // (SIDE * CORES) % SIDE, me // CORES % SIDE, me % CORES
    return (((z + dz) % nz * SIDE + (y + dy) % SIDE) * SIDE + (x + dx) % SIDE) * CORES + (c + dc) % CORES


def _route_pack(n, cap, logits_ref, x_ref, off_ref, send_ref, hot_ref, meta_ref, cnt_ref):
    step = pl.program_id(0)
    tok, experts = logits_ref.shape

    @pl.when(step == 0)
    def _():
        lg = logits_ref[...]
        lane = lax.broadcasted_iota(I32, lg.shape, 1)
        m1 = jnp.max(lg, axis=1, keepdims=True)
        i1 = jnp.min(jnp.where(lg == m1, lane, experts), axis=1, keepdims=True)
        rest = jnp.where(lane == i1, -jnp.inf, lg)
        m2 = jnp.max(rest, axis=1, keepdims=True)
        i2 = jnp.min(jnp.where(rest == m2, lane, experts), axis=1, keepdims=True)
        hot1, hot2 = lane == i1, lane == i2
        chosen = jnp.where(hot1 | hot2, 1.0, 0.0)
        total = jnp.sum(jnp.exp(lg - m1), axis=1, keepdims=True)
        later = lax.broadcasted_iota(I32, (tok, tok), 0)
        early = lax.broadcasted_iota(I32, (tok, tok), 1)
        tri = jnp.where(early < later, 1.0, 0.0).astype(BF16)
        before = jnp.dot(tri, chosen.astype(BF16), preferred_element_type=F32)
        p1 = jnp.sum(jnp.where(hot1, before, 0.0), axis=1, keepdims=True)
        p2 = jnp.sum(jnp.where(hot2, before, 0.0), axis=1, keepdims=True)
        e1, e2 = i1.astype(F32), i2.astype(F32)
        cnt_ref[...] = jnp.sum(chosen, axis=0, keepdims=True)
        table = jnp.zeros_like(lg)
        for k, col in enumerate((1.0 / total, jnp.exp(m2 - m1) / total, e1, e2, p1, p2, e1 * cap + p1, e2 * cap + p2)):
            table = jnp.where(lane == k, col, table)
        meta_ref[...] = table

    off = off_ref[pl.ds(step, 1)].reshape(1, send_ref.shape[0])
    me = lax.axis_index("ep")
    dz, dy, dx, dc = off // (SIDE * SIDE * CORES), off // (SIDE * CORES) % SIDE, off // CORES % SIDE, off % CORES
    other = _device_at(me, n, dz, dy, dx, dc)
    place = lax.broadcasted_iota(I32, off.shape, 1) % cap
    slot = (other * cap + place).astype(F32)
    first = jnp.where(meta_ref[:, 6:7] == slot, 1.0, 0.0)
    second = jnp.where(meta_ref[:, 7:8] == slot, 1.0, 0.0)
    hot_ref[0:tok, :] = first.astype(BF16)
    hot_ref[tok:2 * tok, :] = second.astype(BF16)
    send_ref[...] = lax.dot_general((first + second).astype(BF16), x_ref[...], (((0,), (0,)), ((), ())),
                                    preferred_element_type=F32).astype(BF16)


def _exchange(n, group, send_ref, cnt_ref, hot_hbm, w1_ref, w2_ref, picked_ref, all_ref, got_ref, zh_ref, ret_ref,
              rows, zv, hot, out_sem, got_sem, back_sem, ret_sem, cnt_out, cnt_got, own_sem, load_sem, store_sem):
    me = lax.axis_index("ep")
    order = _send_order(n)
    cap, d_model = send_ref.shape[1:]
    chunks = n // group

    bar = pltpu.get_barrier_semaphore()

    def greet(k, carry):
        pl.semaphore_signal(bar, inc=1, device_id={"ep": (me + k) % n}, device_id_type=MESH)
        return carry

    lax.fori_loop(1, n, greet, 0)
    pl.semaphore_wait(bar, n - 1)

    def span(j):
        return range(j * group, min((j + 1) * group, n - 1))

    def remote(src, dst, out, got, to):
        return pltpu.make_async_remote_copy(src, dst, out, got, device_id={"ep": to}, device_id_type=MESH)

    for j in range(chunks):
        for i in span(j):
            remote(send_ref.at[i], got_ref.at[i], out_sem, got_sem.at[j], _device_at(me, n, *order[i])).start()

    def tell(k, carry):
        remote(cnt_ref, all_ref.at[me], cnt_out, cnt_got, (me + k) % n).start()
        return carry

    lax.fori_loop(1, n, tell, 0)
    own = pltpu.make_async_copy(send_ref.at[n - 1], got_ref.at[n - 1], own_sem)
    own.start()
    own.wait()
    own_cnt = pltpu.make_async_copy(cnt_ref, all_ref.at[me], own_sem)
    own_cnt.start()
    own_cnt.wait()

    def some(j):
        return pl.ds(j * group, group)

    def z_store(j):
        return pltpu.make_async_copy(zv.at[j % 2], zh_ref.at[some(j)], store_sem.at[j % 2])

    def back(j):
        z_store(j).wait()
        for i in span(j):
            dz, dy, dx, dc = order[i]
            to = _device_at(me, n, n - dz, n - dy, n - dx, n - dc)
            remote(zh_ref.at[i], ret_ref.at[i], back_sem, ret_sem.at[j], to).start()

    for j in range(chunks):
        block = got_ref.at[pl.ds(j * group, len(span(j)))]
        pltpu.make_async_copy(block, block, got_sem.at[j]).wait()
        load = pltpu.make_async_copy(got_ref.at[some(j)], rows, load_sem.at[0])
        load.start()
        if j > 0:
            back(j - 1)
        load.wait()
        xs = rows[...].reshape(group * cap, d_model)
        h = jax.nn.gelu(jnp.dot(xs, w1_ref[...], preferred_element_type=F32), approximate=True).astype(BF16)
        z = jnp.dot(h, w2_ref[...], preferred_element_type=F32)
        z = jnp.clip(z, -BF16_MAX, BF16_MAX)
        zv[j % 2] = z.astype(BF16).reshape(group, cap, d_model)
        z_store(j).start()
    back(chunks - 1)
    own_z = pltpu.make_async_copy(zh_ref.at[n - 1], ret_ref.at[n - 1], own_sem)
    own_z.start()
    own_z.wait()

    for j in range(chunks):
        block = ret_ref.at[pl.ds(j * group, len(span(j)))]
        get_hot = pltpu.make_async_copy(hot_hbm.at[j], hot, load_sem.at[1])
        get_hot.start()
        pltpu.make_async_copy(block, block, ret_sem.at[j]).wait()
        load = pltpu.make_async_copy(ret_ref.at[some(j)], rows, load_sem.at[0])
        load.start()
        get_hot.wait()
        load.wait()
        part = jnp.dot(hot[...], rows[...].reshape(group * cap, d_model), preferred_element_type=F32).astype(BF16)
        picked_ref[...] = part if j == 0 else picked_ref[...] + part

    rest = pl.ds(0, n - 1)
    pltpu.make_async_copy(send_ref.at[rest], send_ref.at[rest], out_sem).wait()
    pltpu.make_async_copy(zh_ref.at[rest], zh_ref.at[rest], back_sem).wait()
    pltpu.make_async_copy(all_ref.at[rest], all_ref.at[rest], cnt_out).wait()
    pltpu.make_async_copy(all_ref.at[rest], all_ref.at[rest], cnt_got).wait()


def _finish(capacity, all_ref, x_ref, meta_ref, one_ref, two_ref, out_ref):
    me = lax.axis_index("ep")
    early = lax.broadcasted_iota(I32, all_ref.shape, 0) < me
    base = jnp.sum(jnp.where(early, all_ref[...], 0.0), axis=0)
    meta = meta_ref[...]
    lane = lax.broadcasted_iota(I32, meta.shape, 1).astype(F32)
    y = 0.0
    for k, z_ref in enumerate((one_ref, two_ref)):
        e, pos = meta[:, 2 + k:3 + k], meta[:, 4 + k:5 + k]
        before = pos + jnp.sum(jnp.where(lane == e, base, 0.0), axis=1, keepdims=True)
        y += jnp.where(before < capacity, meta[:, k:k + 1], 0.0) * z_ref[...].astype(F32)
    out_ref[...] = (x_ref[...].astype(F32) + y).astype(BF16)


def solution(mesh):
    n = mesh.shape["ep"]
    row_spec = P(("dp", "ep"), None)
    expert_spec = P("ep", None, None)

    def local_step(x_rows, logits, w_in, w_out):
        tok, d_model = x_rows.shape
        experts = logits.shape[1]
        capacity = CAP_FACTOR * tok * n // experts
        cap = 4 * tok // experts
        group = 16
        chunks, width = n // group, group * cap
        code = np.array([((z * SIDE + y) * SIDE + x) * CORES + c for z, y, x, c in _send_order(n)], np.int32)
        offsets = jnp.asarray(np.repeat(code, cap).reshape(chunks, 1, width))
        whole = lambda *s: pl.BlockSpec(s, lambda i: (0,) * len(s))
        send, hot, meta, cnt = pl.pallas_call(
            functools.partial(_route_pack, n, cap),
            grid=(chunks,),
            in_specs=[whole(tok, experts), whole(tok, d_model), whole(chunks, 1, width)],
            out_specs=[pl.BlockSpec((width, d_model), lambda i: (i, 0)), pl.BlockSpec((2 * tok, width), lambda i: (i, 0)),
                       whole(tok, experts), whole(1, experts)],
            out_shape=[jax.ShapeDtypeStruct((chunks * width, d_model), BF16),
                       jax.ShapeDtypeStruct((chunks * 2 * tok, width), BF16),
                       jax.ShapeDtypeStruct((tok, experts), F32), jax.ShapeDtypeStruct((1, experts), F32)],
            name="route_pack",
        )(logits, x_rows, offsets)

        any_ = pl.BlockSpec(memory_space=pl.ANY)
        vmem = pl.BlockSpec(memory_space=pltpu.VMEM)
        dma = pltpu.SemaphoreType.DMA
        slab = jax.ShapeDtypeStruct((n, cap, d_model), BF16)
        picked, all_cnt = pl.pallas_call(
            functools.partial(_exchange, n, group),
            in_specs=[any_, any_, any_, vmem, vmem],
            out_specs=[vmem, any_, any_, any_, any_],
            out_shape=[jax.ShapeDtypeStruct((2 * tok, d_model), BF16), jax.ShapeDtypeStruct((n, 1, experts), F32),
                       slab, slab, slab],
            scratch_shapes=[pltpu.VMEM((group, cap, d_model), BF16), pltpu.VMEM((2, group, cap, d_model), BF16),
                            pltpu.VMEM((2 * tok, width), BF16),
                            dma, dma((chunks,)), dma, dma((chunks,)), dma, dma, dma, dma((2,)), dma((2,))],
            compiler_params=pltpu.CompilerParams(collective_id=0, has_side_effects=True, vmem_limit_bytes=60 * 2**20),
            name="exchange",
        )(send.reshape(n, cap, d_model), cnt, hot.reshape(chunks, 2 * tok, width), w_in[0], w_out[0])[:2]

        blk = tok // 4
        part = lambda s: pl.BlockSpec((blk, d_model), lambda i: (i + s, 0))
        return pl.pallas_call(
            functools.partial(_finish, capacity),
            grid=(tok // blk,),
            in_specs=[whole(n, 1, experts), part(0), pl.BlockSpec((blk, experts), lambda i: (i, 0)), part(0),
                      part(tok // blk)],
            out_specs=part(0),
            out_shape=jax.ShapeDtypeStruct((tok, d_model), BF16),
            name="finish",
        )(all_cnt, x_rows, meta, picked, picked)

    return jax.shard_map(local_step, mesh=mesh, in_specs=(row_spec, row_spec, expert_spec, expert_spec),
                         out_specs=row_spec, check_vma=False)
```

time: 276 us -> 271 us (0.982)
  the two profiles are of different devices: /device:TPU:4 before, /device:TPU:87 now
where the time goes in v4:
time: 271 us; the launch traced here: 270 us
  Pallas kernels  270 us (100%)
    pallas_call x1, Pallas kernels, local_step(): pl.pallas_call(functools.partial(_exchange, n, group), in_specs=[any_, an...  252 us
    pallas_call x1, Pallas kernels, local_step(): pl.pallas_call(functools.partial(_route_pack, n, cap), grid=(chunks,), in...  12 us
    pallas_call x1, Pallas kernels, local_step(): pl.pallas_call(functools.partial(_finish, capacity), grid=(tok // blk,),...  5.93 us

profile of v4, /device:TPU:87, one launch (start us, length us, event | category | flops | bytes accessed | tf_op | source)
XLA Modules:
  0.0 269.8 jit_solution(16051054660233101465)
XLA Ops:
  0.0 12.0 %route_pack.1 = (bf16[2048,2048]{1,0:T(8,128)(2,1)}, bf16[8192,256]{1,0:T(8,128)(2,1)}, f32[512,128]{1,0:T(8,128)}, f32[1,128]{1,0:T(1,128)}) custom-call(f32[512,128]{1,0:T(8,128)} %logits_ref.1, bf16[512,2048]{1,0:T(8,128)(2,1)} %x_ref.3, s32[8,1,256]{2,1,0:T(1,128)} %constant.2.clone.off_ref), custom_call_target="tpu_custom_call" | custom-call | tf_op jit(solution)/shard_map/route_pack/pallas_call | solution.py:201
  12.0 251.9 %exchange.1 = (bf16[1024,2048]{1,0:T(8,128)(2,1)}, f32[128,1,128]{2,1,0:T(1,128)}, bf16[128,16,2048]{2,1,0:T(8,128)(2,1)}, bf16[128,16,2048]{2,1,0:T(8,128)(2,1)}, bf16[128,16,2048]{2,1,0:T(8,128)(2,1)}) custom-call(bf16[128,16,2048]{2,1,0:T(8,128)(2,1)} %bitcast.4, f32[1,128]{1,0:T(1,128)} %get-tuple-element.12.cnt_ref, bf16[8,1024,256]{2,1,0:T(8,128)(2,1)} %bitcast.5, ...), custom_call_target="tpu_custom_call" | custom-call | tf_op jit(solution)/shard_map/exchange/pallas_call | solution.py:217
  263.9 5.9 %finish.1 = bf16[512,2048]{1,0:T(8,128)(2,1)} custom-call(f32[128,1,128]{2,1,0:T(1,128)} %get-tuple-element.14.all_ref, bf16[512,2048]{1,0:T(8,128)(2,1)} %x_ref.3, f32[512,128]{1,0:T(8,128)} %get-tuple-element.15.meta_ref, bf16[1024,2048]{1,0:T(8,128)(2,1)} %get-tuple-element.16.one_ref.two_ref, bf16[1024,2048]{1,0:T(8,128)(2,1)} %get-tuple-element.16.one_ref.two_ref), custom_call_target="tpu_custom_call" | custom-call | tf_op jit(solution)/shard_map/finish/pallas_call | solution.py:232

commit v5 on v2

v5 whole, which is shorter than its diff:
```python
import functools
import jax
import jax.numpy as jnp
from jax import lax
from jax.experimental import pallas as pl
from jax.experimental.pallas import tpu as pltpu
from jax.sharding import PartitionSpec as P

CAP_FACTOR = 2
HALVES = 2
F32, BF16 = jnp.float32, jnp.bfloat16
MESH = pl.DeviceIdType.MESH
BF16_MAX = float(jnp.finfo(jnp.bfloat16).max)


def _grid_dims(n):
    return n // 32, 4, 4, 2


def _peer(me, n, i, sign):
    p = n - 1
    square = i * i % p
    k = square * square % p * i % p + 1
    nz, ny, nx, nc = _grid_dims(n)
    dz, dy, dx, dc = k // (ny * nx * nc), (k // (nx * nc)) % ny, (k // nc) % nx, k % nc
    if sign < 0:
        dz, dy, dx = nz - dz, ny - dy, nx - dx
    z, y, x, c = me // (ny * nx * nc), (me // (nx * nc)) % ny, (me // nc) % nx, me % nc
    return (((z + dz) % nz * ny + (y + dy) % ny) * nx + (x + dx) % nx) * nc + (c + dc) % nc


def _route_pack(src_cap, logits_ref, x_ref, send_ref, meta_ref, cnt_ref, slot_row):
    step = pl.program_id(0)

    @pl.when(step == 0)
    def _():
        lg = logits_ref[...]
        tok, experts = lg.shape
        lane = lax.broadcasted_iota(jnp.int32, lg.shape, 1)
        m1 = jnp.max(lg, axis=1, keepdims=True)
        i1 = jnp.min(jnp.where(lg == m1, lane, experts), axis=1, keepdims=True)
        rest = jnp.where(lane == i1, -jnp.inf, lg)
        m2 = jnp.max(rest, axis=1, keepdims=True)
        i2 = jnp.min(jnp.where(rest == m2, lane, experts), axis=1, keepdims=True)
        hot1, hot2 = lane == i1, lane == i2
        chosen = jnp.where(hot1 | hot2, 1.0, 0.0)
        total = jnp.sum(jnp.exp(lg - m1), axis=1, keepdims=True)
        g1 = 1.0 / total
        g2 = jnp.exp(m2 - m1) / total
        later = lax.broadcasted_iota(jnp.int32, (tok, tok), 0)
        early = lax.broadcasted_iota(jnp.int32, (tok, tok), 1)
        tri = jnp.where(early < later, 1.0, 0.0).astype(BF16)
        before = jnp.dot(tri, chosen.astype(BF16), preferred_element_type=F32)
        p1 = jnp.sum(jnp.where(hot1, before, 0.0), axis=1, keepdims=True)
        p2 = jnp.sum(jnp.where(hot2, before, 0.0), axis=1, keepdims=True)
        cnt_ref[...] = jnp.sum(chosen, axis=0, keepdims=True)
        e1, e2 = i1.astype(F32), i2.astype(F32)
        part = src_cap // HALVES

        def slot_of(e, p):
            half = jnp.where(p >= part, 1.0, 0.0)
            return half * (experts * part) + e * part + p - half * part

        meta = jnp.where(lane == 0, g1, jnp.where(lane == 1, g2, jnp.where(lane == 2, e1, jnp.where(
            lane == 3, e2, jnp.where(lane == 4, p1, jnp.where(lane == 5, p2, jnp.where(
                lane == 6, slot_of(e1, p1), jnp.where(lane == 7, slot_of(e2, p2), 0.0))))))))
        meta_ref[...] = meta
        slot_row[...] = meta.T[0:8, :].astype(jnp.int32)

    rows = send_ref.shape[0]
    slot = lax.broadcasted_iota(jnp.int32, (rows, x_ref.shape[0]), 0) + step * rows
    pick = (slot == slot_row[6:7, :]) | (slot == slot_row[7:8, :])
    hot = jnp.where(pick, 1.0, 0.0).astype(BF16)
    send_ref[...] = jnp.dot(hot, x_ref[...], preferred_element_type=F32).astype(BF16)


def _exchange(n, group, send_ref, cnt_ref, w1_ref, w2_ref, ret_ref, all_ref, got_ref, zh_ref, rows, zv,
              out_sem, got_sem, back_sem, ret_sem, cnt_out, cnt_got, own_sem, load_sem, store_sem):
    me = lax.axis_index("ep")
    part, d_model = send_ref.shape[2:]
    chunks = n // group

    bar = pltpu.get_barrier_semaphore()

    def greet(k, carry):
        pl.semaphore_signal(bar, inc=1, device_id={"ep": (me + k) % n}, device_id_type=MESH)
        return carry

    lax.fori_loop(1, n, greet, 0)
    pl.semaphore_wait(bar, n - 1)

    def span(c):
        return range(c * group, min((c + 1) * group, n - 1))

    todo = [(h, c) for h in range(HALVES) for c in range(chunks)]
    for j, (h, c) in enumerate(todo):

        def send(i, carry):
            peer = _peer(me, n, i, 1)
            pltpu.make_async_remote_copy(send_ref.at[h, peer], got_ref.at[h, i], out_sem.at[h], got_sem.at[j],
                                         device_id={"ep": peer}, device_id_type=MESH).start()
            return carry

        lax.fori_loop(span(c).start, span(c).stop, send, 0)

    def tell(k, carry):
        pltpu.make_async_remote_copy(cnt_ref, all_ref.at[me], cnt_out, cnt_got, device_id={"ep": (me + k) % n},
                                     device_id_type=MESH).start()
        return carry

    lax.fori_loop(1, n, tell, 0)
    for h in range(HALVES):
        own = pltpu.make_async_copy(send_ref.at[h, me], got_ref.at[h, n - 1], own_sem)
        own.start()
        own.wait()
    own_cnt = pltpu.make_async_copy(cnt_ref, all_ref.at[me], own_sem)
    own_cnt.start()
    own_cnt.wait()

    def z_store(j):
        h, c = todo[j]
        return pltpu.make_async_copy(zv.at[j % 2], zh_ref.at[h, pl.ds(c * group, group)], store_sem.at[j % 2])

    def back(j):
        h, c = todo[j]
        z_store(j).wait()

        def give(i, carry):
            pltpu.make_async_remote_copy(zh_ref.at[h, i], ret_ref.at[h, me], back_sem.at[h], ret_sem.at[h],
                                         device_id={"ep": _peer(me, n, i, -1)}, device_id_type=MESH).start()
            return carry

        lax.fori_loop(span(c).start, span(c).stop, give, 0)

    for j, (h, c) in enumerate(todo):
        block = got_ref.at[h, pl.ds(c * group, len(span(c)))]
        pltpu.make_async_copy(block, block, got_sem.at[j]).wait()
        load = pltpu.make_async_copy(got_ref.at[h, pl.ds(c * group, group)], rows, load_sem)
        load.start()
        if j > 0:
            back(j - 1)
        load.wait()
        xs = rows[...].reshape(group * part, d_model)
        hid = jax.nn.gelu(jnp.dot(xs, w1_ref[...], preferred_element_type=F32), approximate=True).astype(BF16)
        z = jnp.dot(hid, w2_ref[...], preferred_element_type=F32)
        z = jnp.clip(z, -BF16_MAX, BF16_MAX)
        zv[j % 2] = z.astype(BF16).reshape(group, part, d_model)
        z_store(j).start()
    back(len(todo) - 1)
    for h in range(HALVES):
        own_z = pltpu.make_async_copy(zh_ref.at[h, n - 1], ret_ref.at[h, me], own_sem)
        own_z.start()
        own_z.wait()

    rest = pl.ds(0, n - 1)
    for h in range(HALVES):
        pltpu.make_async_copy(send_ref.at[h, rest], send_ref.at[h, rest], out_sem.at[h]).wait()
        pltpu.make_async_copy(zh_ref.at[h, rest], zh_ref.at[h, rest], back_sem.at[h]).wait()
    pltpu.make_async_copy(all_ref.at[rest], all_ref.at[rest], cnt_out).wait()
    pltpu.make_async_copy(all_ref.at[rest], all_ref.at[rest], cnt_got).wait()
    for h in range(HALVES):
        pltpu.make_async_copy(ret_ref.at[h, rest], ret_ref.at[h, rest], ret_sem.at[h]).wait()


def _combine(capacity, all_ref, ret_ref, x_ref, meta_ref, out_ref, pick):
    tok = x_ref.shape[0]

    @pl.when(pl.program_id(0) == 0)
    def _():
        meta = meta_ref[...]
        before_me = lax.broadcasted_iota(jnp.int32, all_ref.shape, 0) < lax.axis_index("ep")
        base = jnp.sum(jnp.where(before_me, all_ref[...], 0.0), axis=0)
        lane = lax.broadcasted_iota(jnp.int32, meta.shape, 1).astype(F32)
        slots = lax.broadcasted_iota(jnp.int32, (tok, pick.shape[1]), 1).astype(F32)
        for c in range(2):
            e, pos, slot = meta[:, 2 + c:3 + c], meta[:, 4 + c:5 + c], meta[:, 6 + c:7 + c]
            ahead = jnp.sum(jnp.where(lane == e, base, 0.0), axis=1, keepdims=True)
            slot = jnp.where(pos + ahead < capacity, slot, -1.0)
            pick[c * tok:(c + 1) * tok, :] = jnp.where(slots == slot, 1.0, 0.0).astype(BF16)

    z = ret_ref[...]
    z = jnp.where(z == z, z, jnp.zeros_like(z))
    r = jnp.dot(pick[...], z, preferred_element_type=F32)
    y = meta_ref[:, 0:1] * r[0:tok] + meta_ref[:, 1:2] * r[tok:2 * tok]
    out_ref[...] = (x_ref[...].astype(F32) + y).astype(BF16)


def solution(mesh):
    n = mesh.shape["ep"]
    row_spec = P(("dp", "ep"), None)
    expert_spec = P("ep", None, None)

    def local_step(x_rows, logits, w_in, w_out):
        tok, d_model = x_rows.shape
        experts = logits.shape[1]
        ff = w_in.shape[2]
        capacity = CAP_FACTOR * tok * n // experts
        src_cap = 4 * tok // experts
        slots = experts * src_cap
        blk = 256
        whole = lambda *s: pl.BlockSpec(s, lambda i: (0,) * len(s))
        send, meta, cnt = pl.pallas_call(
            functools.partial(_route_pack, src_cap),
            grid=(slots // blk,),
            in_specs=[whole(tok, experts), whole(tok, d_model)],
            out_specs=[pl.BlockSpec((blk, d_model), lambda i: (i, 0)), whole(tok, experts), whole(1, experts)],
            out_shape=[jax.ShapeDtypeStruct((slots, d_model), BF16), jax.ShapeDtypeStruct((tok, experts), F32),
                       jax.ShapeDtypeStruct((1, experts), F32)],
            scratch_shapes=[pltpu.VMEM((8, tok), jnp.int32)],
            name="route_pack",
        )(logits, x_rows)

        group = 32
        part = src_cap // HALVES
        slab = jax.ShapeDtypeStruct((HALVES, n, part, d_model), BF16)
        any_ = pl.BlockSpec(memory_space=pl.ANY)
        vmem = pl.BlockSpec(memory_space=pltpu.VMEM)
        dma = pltpu.SemaphoreType.DMA
        ret, all_cnt, _, _ = pl.pallas_call(
            functools.partial(_exchange, n, group),
            in_specs=[any_, any_, vmem, vmem],
            out_specs=[any_, any_, any_, any_],
            out_shape=[slab, jax.ShapeDtypeStruct((n, 1, experts), F32),
                       slab,
                       slab],
            scratch_shapes=[pltpu.VMEM((group, part, d_model), BF16), pltpu.VMEM((2, group, part, d_model), BF16),
                            dma((HALVES,)), dma((HALVES * n // group,)), dma((HALVES,)), dma((HALVES,)), dma, dma, dma, dma, dma((2,))],
            compiler_params=pltpu.CompilerParams(collective_id=0, has_side_effects=True, vmem_limit_bytes=60 * 2**20),
            name="exchange",
        )(send.reshape(HALVES, n, part, d_model), cnt, w_in[0], w_out[0])

        cols = 256
        return pl.pallas_call(
            functools.partial(_combine, capacity),
            grid=(d_model // cols,),
            in_specs=[whole(n, 1, experts), pl.BlockSpec((slots, cols), lambda i: (0, i)),
                      pl.BlockSpec((tok, cols), lambda i: (0, i)), whole(tok, experts)],
            out_specs=pl.BlockSpec((tok, cols), lambda i: (0, i)),
            out_shape=jax.ShapeDtypeStruct((tok, d_model), BF16),
            scratch_shapes=[pltpu.VMEM((2 * tok, slots), BF16)],
            name="combine",
        )(all_cnt, ret.reshape(slots, d_model), x_rows, meta)

    return jax.shard_map(local_step, mesh=mesh, in_specs=(row_spec, row_spec, expert_spec, expert_spec),
                         out_specs=row_spec, check_vma=False)
```

time: 269 us -> 269 us (level)
  the two profiles are of different devices: /device:TPU:16 before, /device:TPU:99 now
where the time goes in v5:
time: 269 us
  Pallas kernels  269 us (100%)
    pallas_call x1, Pallas kernels, local_step(): pl.pallas_call(functools.partial(_exchange, n, group), in_specs=[any_, an...  244 us
    pallas_call x1, Pallas kernels, local_step(): pl.pallas_call(functools.partial(_combine, capacity), grid=(d_model // co...  13.9 us
    pallas_call x1, Pallas kernels, local_step(): pl.pallas_call(functools.partial(_route_pack, src_cap), grid=(slots // bl...  10.5 us

profile of v5, /device:TPU:99, one launch (start us, length us, event | category | flops | bytes accessed | tf_op | source)
XLA Modules:
  0.0 268.8 jit_solution(7681903813750964556)
XLA Ops:
  0.0 10.5 %route_pack.1 = (bf16[2048,2048]{1,0:T(8,128)(2,1)}, f32[512,128]{1,0:T(8,128)}, f32[1,128]{1,0:T(1,128)}) custom-call(f32[512,128]{1,0:T(8,128)} %logits_ref.1, bf16[512,2048]{1,0:T(8,128)(2,1)} %x_ref.3), custom_call_target="tpu_custom_call" | custom-call | tf_op jit(solution)/shard_map/route_pack/pallas_call | solution.py:202
  10.5 244.4 %exchange.1 = (bf16[2,128,8,2048]{3,2,1,0:T(8,128)(2,1)}, f32[128,1,128]{2,1,0:T(1,128)}, bf16[2,128,8,2048]{3,2,1,0:T(8,128)(2,1)}, bf16[2,128,8,2048]{3,2,1,0:T(8,128)(2,1)}) custom-call(bf16[2,128,8,2048]{3,2,1,0:T(8,128)(2,1)} %bitcast.4, f32[1,128]{1,0:T(1,128)} %get-tuple-element.11.cnt_ref, bf16[2048,768]{1,0:T(8,128)(2,1)} %bitcast.6, ...), custom_call_target="tpu_custom_call" | custom-call | tf_op jit(solution)/shard_map/exchange/pallas_call | solution.py:219
  254.9 13.9 %combine.1 = bf16[512,2048]{1,0:T(8,128)(2,1)} custom-call(f32[128,1,128]{2,1,0:T(1,128)} %get-tuple-element.12.all_ref, bf16[2048,2048]{1,0:T(8,128)(2,1)} %bitcast.5, bf16[512,2048]{1,0:T(8,128)(2,1)} %x_ref.3, f32[512,128]{1,0:T(8,128)} %get-tuple-element.14.meta_ref), custom_call_target="tpu_custom_call" | custom-call | tf_op jit(solution)/shard_map/combine/pallas_call | solution.py:233

commit v6 on v5

--- a/solution.py
+++ b/solution.py
@@ -29,7 +29,7 @@
     return (((z + dz) % nz * ny + (y + dy) % ny) * nx + (x + dx) % nx) * nc + (c + dc) % nc
 
 
-def _route_pack(src_cap, logits_ref, x_ref, send_ref, meta_ref, cnt_ref, slot_row):
+def _route(src_cap, logits_ref, pick_ref, meta_ref, cnt_ref, slot_row):
     step = pl.program_id(0)
 
     @pl.when(step == 0)
@@ -67,14 +67,13 @@
         meta_ref[...] = meta
         slot_row[...] = meta.T[0:8, :].astype(jnp.int32)
 
-    rows = send_ref.shape[0]
-    slot = lax.broadcasted_iota(jnp.int32, (rows, x_ref.shape[0]), 0) + step * rows
+    rows, tok = pick_ref.shape
+    slot = lax.broadcasted_iota(jnp.int32, (rows, tok), 0) + step * rows
     pick = (slot == slot_row[6:7, :]) | (slot == slot_row[7:8, :])
-    hot = jnp.where(pick, 1.0, 0.0).astype(BF16)
-    send_ref[...] = jnp.dot(hot, x_ref[...], preferred_element_type=F32).astype(BF16)
-
-
-def _exchange(n, group, send_ref, cnt_ref, w1_ref, w2_ref, ret_ref, all_ref, got_ref, zh_ref, rows, zv,
+    pick_ref[...] = jnp.where(pick, 1.0, 0.0).astype(BF16)
+
+
+def _exchange(n, group, pick_ref, x_ref, cnt_ref, w1_ref, w2_ref, ret_ref, all_ref, send_ref, got_ref, zh_ref, rows, zv,
               out_sem, got_sem, back_sem, ret_sem, cnt_out, cnt_got, own_sem, load_sem, store_sem):
     me = lax.axis_index("ep")
     part, d_model = send_ref.shape[2:]
@@ -87,21 +86,38 @@
         return carry
 
     lax.fori_loop(1, n, greet, 0)
-    pl.semaphore_wait(bar, n - 1)
 
     def span(c):
         return range(c * group, min((c + 1) * group, n - 1))
 
     todo = [(h, c) for h in range(HALVES) for c in range(chunks)]
+
+    def pack(j):
+        h, c = todo[j]
+        return pltpu.make_async_copy(zv.at[j % 2], send_ref.at[h, pl.ds(c * group, group)], store_sem.at[j % 2])
+
+    width = group * part
     for j, (h, c) in enumerate(todo):
-
-        def send(i, carry):
+        if c >= 2:
+            pack(j - 2).wait()
+        rows_now = jnp.dot(pick_ref[j * width:(j + 1) * width, :], x_ref[...], preferred_element_type=F32)
+        zv[j % 2] = rows_now.astype(BF16).reshape(group, part, d_model)
+        pack(j).start()
+        if c < chunks - 1:
+            continue
+        if h == 0:
+            pl.semaphore_wait(bar, n - 1)
+        pack(j - 1).wait()
+        pack(j).wait()
+
+        def send(at, i, carry, h=h):
             peer = _peer(me, n, i, 1)
-            pltpu.make_async_remote_copy(send_ref.at[h, peer], got_ref.at[h, i], out_sem.at[h], got_sem.at[j],
+            pltpu.make_async_remote_copy(send_ref.at[h, peer], got_ref.at[h, i], out_sem.at[h], got_sem.at[at],
                                          device_id={"ep": peer}, device_id_type=MESH).start()
             return carry
 
-        lax.fori_loop(span(c).start, span(c).stop, send, 0)
+        for k in range(chunks):
+            lax.fori_loop(span(k).start, span(k).stop, functools.partial(send, h * chunks + k), 0)
 
     def tell(k, carry):
         pltpu.make_async_remote_copy(cnt_ref, all_ref.at[me], cnt_out, cnt_got, device_id={"ep": (me + k) % n},
@@ -199,16 +215,16 @@
         slots = experts * src_cap
         blk = 256
         whole = lambda *s: pl.BlockSpec(s, lambda i: (0,) * len(s))
-        send, meta, cnt = pl.pallas_call(
-            functools.partial(_route_pack, src_cap),
+        pick, meta, cnt = pl.pallas_call(
+            functools.partial(_route, src_cap),
             grid=(slots // blk,),
-            in_specs=[whole(tok, experts), whole(tok, d_model)],
-            out_specs=[pl.BlockSpec((blk, d_model), lambda i: (i, 0)), whole(tok, experts), whole(1, experts)],
-            out_shape=[jax.ShapeDtypeStruct((slots, d_model), BF16), jax.ShapeDtypeStruct((tok, experts), F32),
+            in_specs=[whole(tok, experts)],
+            out_specs=[pl.BlockSpec((blk, tok), lambda i: (i, 0)), whole(tok, experts), whole(1, experts)],
+            out_shape=[jax.ShapeDtypeStruct((slots, tok), BF16), jax.ShapeDtypeStruct((tok, experts), F32),
                        jax.ShapeDtypeStruct((1, experts), F32)],
             scratch_shapes=[pltpu.VMEM((8, tok), jnp.int32)],
-            name="route_pack",
-        )(logits, x_rows)
+            name="route",
+        )(logits)
 
         group = 32
         part = src_cap // HALVES
@@ -216,18 +232,18 @@
         any_ = pl.BlockSpec(memory_space=pl.ANY)
         vmem = pl.BlockSpec(memory_space=pltpu.VMEM)
         dma = pltpu.SemaphoreType.DMA
-        ret, all_cnt, _, _ = pl.pallas_call(
+        ret, all_cnt = pl.pallas_call(
             functools.partial(_exchange, n, group),
-            in_specs=[any_, any_, vmem, vmem],
-            out_specs=[any_, any_, any_, any_],
+            in_specs=[vmem, vmem, any_, vmem, vmem],
+            out_specs=[any_, any_, any_, any_, any_],
             out_shape=[slab, jax.ShapeDtypeStruct((n, 1, experts), F32),
                        slab,
-                       slab],
+                       slab, slab],
             scratch_shapes=[pltpu.VMEM((group, part, d_model), BF16), pltpu.VMEM((2, group, part, d_model), BF16),
                             dma((HALVES,)), dma((HALVES * n // group,)), dma((HALVES,)), dma((HALVES,)), dma, dma, dma, dma, dma((2,))],
             compiler_params=pltpu.CompilerParams(collective_id=0, has_side_effects=True, vmem_limit_bytes=60 * 2**20),
             name="exchange",
-        )(send.reshape(HALVES, n, part, d_model), cnt, w_in[0], w_out[0])
+        )(pick, x_rows, cnt, w_in[0], w_out[0])[:2]
 
         cols = 256
         return pl.pallas_call(

time: 269 us -> 252 us (0.937)
  the two profiles are of different devices: /device:TPU:99 before, /device:TPU:35 now
where the time goes in v6:
time: 252 us; the launch traced here: 251 us
  Pallas kernels  251 us (100%)
    pallas_call x1, Pallas kernels, local_step(): pl.pallas_call(functools.partial(_exchange, n, group), in_specs=[vmem, vm...  232 us
    pallas_call x1, Pallas kernels, local_step(): pl.pallas_call(functools.partial(_combine, capacity), grid=(d_model // co...  13.9 us
    pallas_call x1, Pallas kernels, local_step(): pl.pallas_call(functools.partial(_route, src_cap), grid=(slots // blk,),...  5.44 us

profile of v6, /device:TPU:35, one launch (start us, length us, event | category | flops | bytes accessed | tf_op | source)
XLA Modules:
  0.0 251.1 jit_solution(13367211798035547423)
XLA Ops:
  0.0 5.4 %route.1 = (bf16[2048,512]{1,0:T(8,128)(2,1)}, f32[512,128]{1,0:T(8,128)}, f32[1,128]{1,0:T(1,128)}) custom-call(f32[512,128]{1,0:T(8,128)} %logits_ref.1), custom_call_target="tpu_custom_call" | custom-call | tf_op jit(solution)/shard_map/route/pallas_call | solution.py:218
  5.4 231.7 %exchange.1 = (bf16[2,128,8,2048]{3,2,1,0:T(8,128)(2,1)}, f32[128,1,128]{2,1,0:T(1,128)}, bf16[2,128,8,2048]{3,2,1,0:T(8,128)(2,1)}, bf16[2,128,8,2048]{3,2,1,0:T(8,128)(2,1)}, bf16[2,128,8,2048]{3,2,1,0:T(8,128)(2,1)}) custom-call(bf16[2048,512]{1,0:T(8,128)(2,1)} %get-tuple-element.10.pick_ref, bf16[512,2048]{1,0:T(8,128)(2,1)} %x_ref.3, ...), custom_call_target="tpu_custom_call" | custom-call | tf_op jit(solution)/shard_map/exchange/pallas_call | solution.py:235
  237.2 13.9 %combine.1 = bf16[512,2048]{1,0:T(8,128)(2,1)} custom-call(f32[128,1,128]{2,1,0:T(1,128)} %get-tuple-element.12.all_ref, bf16[2048,2048]{1,0:T(8,128)(2,1)} %bitcast.3, bf16[512,2048]{1,0:T(8,128)(2,1)} %x_ref.3, f32[512,128]{1,0:T(8,128)} %get-tuple-element.14.meta_ref), custom_call_target="tpu_custom_call" | custom-call | tf_op jit(solution)/shard_map/combine/pallas_call | solution.py:249
